TPU v7x, 32 devices: a whole 2x2x4 slice. The times are simulated.
32 devices in a mesh: row: 8 (over y, x, core), col: 4 (over z).
Axes of the slice: x: 2, y: 2, z: 4, core: 2. Of those that a mesh axis runs over, the one named last changes fastest.
Arguments:
- positions: float32 [3, 16384], P(None, ('row', 'col')), may hold values from -6 to 6
- velocities: float32 [3, 16384], P(None, ('row', 'col')), may hold values from -6 to 6
- accels: float32 [3, 16384], P(None, ('row', 'col')), may hold values from -0.75 to 0.75
- jerks: float32 [3, 16384], P(None, ('row', 'col')), may hold values from -1.5 to 1.5
- masses: float32 [16384], P(('row', 'col')), may hold values from 0.3 to 3
- elapsed: float32 [16384], P(('row', 'col')), may hold values from 0.05 to 0.5
- active_star: int32 [1024], replicated, may hold values from 0 to 16383, as said below
Outputs:
- new_positions: float32 [3, 16384], P(None, ('row', 'col'))
- new_velocities: float32 [3, 16384], P(None, ('row', 'col'))
- new_accels: float32 [3, 16384], P(None, ('row', 'col'))
- new_jerks: float32 [3, 16384], P(None, ('row', 'col'))
Inputs may be any that keep to these rules, and one draw needn't show every extreme that they name: `active_star`: the 1024 ids are distinct. Star g is owned by device g // 512, devices counted with row slowest and col fastest. In each aligned block of 128 entries (one group of targets), at most 48 entries name stars whose owning device has the same col index, and in every block some col index has exactly 48.
All inputs are finite; a program needn't handle non-finite values.
Results may differ from a plain program's by a relative error of at most 0.0003.
Values sent between devices are 32-bit elements; how exact they have to be, the bound alone decides.
No kernel may reach another device: no remote copies, remote signals or barrier semaphores. Data moves between devices by JAX's collectives and lax.ppermute only.
A program may use at most 64 MiB of HBM per device.

v0:
```python
import functools

import jax
import jax.numpy as jnp
from jax import lax
from jax.experimental import pallas as pl
from jax.experimental.pallas import tpu as pltpu
from jax.sharding import PartitionSpec as P


softening = 0.001
LANES = 128
SUB = 8
AXES = ("row", "col")
VMEM = pl.BlockSpec(memory_space=pltpu.VMEM)
SMEM = pl.BlockSpec(memory_space=pltpu.SMEM)


PARAMS = pltpu.CompilerParams(vmem_limit_bytes=4 << 20)


def near(value):
    return pltpu.with_memory_space_constraint(value, pltpu.VMEM)


def far(value):
    return pltpu.with_memory_space_constraint(value, pltpu.HBM)


def predict_body(pos, vel, acc, jerk, mass, elapsed, out):
    step = elapsed[...]
    moved_pos = pos[...] + step * (vel[...] + step * (0.5 * acc[...] + step * jerk[...] * (1.0 / 6.0)))
    moved_vel = vel[...] + step * (acc[...] + 0.5 * step * jerk[...])
    for tile in range(pos.shape[1] // LANES):
        lanes = slice(tile * LANES, (tile + 1) * LANES)
        out[7 * tile : 7 * tile + 3, :] = moved_pos[:, lanes]
        out[7 * tile + 3 : 7 * tile + 6, :] = moved_vel[:, lanes]
        out[7 * tile + 6 : 7 * tile + 7, :] = mass[:, lanes]


def splat_row(ref, row):
    return jnp.broadcast_to(ref[row : row + 1, :], (SUB, LANES))


def add_pairs(target, sums, source):
    sums = list(sums)
    for base in range(0, source.shape[0], 7):
        sep = [splat_row(source, base + k) - target[k] for k in range(3)]
        rel = [splat_row(source, base + 3 + k) - target[3 + k] for k in range(3)]
        radius_sq = (sep[0] * sep[0] + sep[1] * sep[1]) + (sep[2] * sep[2] + softening)
        inverse = lax.rsqrt(radius_sq)
        inverse_sq = inverse * inverse
        weight = (splat_row(source, base + 6) * inverse) * inverse_sq
        dot = (sep[0] * rel[0] + sep[1] * rel[1]) + sep[2] * rel[2]
        closing = (3.0 * inverse_sq) * dot
        for k in range(3):
            sums[k] = sums[k] + weight * sep[k]
            sums[3 + k] = sums[3 + k] + weight * (rel[k] - closing * sep[k])
    return sums


def zeros6():
    return [jnp.zeros((SUB, LANES), jnp.float32) for _ in range(6)]


def setup_body(base, active, own, count, rank, targets, sums):
    tiles = own.shape[0] // 7
    rows = max(SUB, tiles)
    sub_rows = lax.broadcasted_iota(jnp.int32, (rows, LANES), 0)
    sub_lanes = lax.broadcasted_iota(jnp.int32, (LANES, LANES), 0)
    lane_cols = lax.broadcasted_iota(jnp.int32, (LANES, LANES), 1)
    flags = jnp.zeros((rows, LANES), jnp.float32)
    for r in range(active.shape[0]):
        local = active[r : r + 1, :] - base[0]
        high = local >> 7
        high = jnp.where(high < tiles, high, -1)
        low = local & 127
        one = (sub_rows == high).astype(jnp.float32)
        two = (sub_lanes == low).astype(jnp.float32)
        flags = flags + lax.dot_general(
            one, two, (((1,), (1,)), ((), ())), preferred_element_type=jnp.float32
        )
    before = (sub_lanes < lane_cols).astype(jnp.float32)
    order = jnp.dot(flags, before, preferred_element_type=jnp.float32)
    in_row = jnp.sum(flags, axis=1, keepdims=True)
    for r in range(tiles - 1):
        order = order + jnp.where(sub_rows > r, in_row[r : r + 1, :], 0.0)
    rank[...] = jnp.where(flags > 0.5, order, -1.0)
    total = jnp.sum(flags).astype(jnp.int32)
    count[0] = (total + (SUB - 1)) // SUB
    slot = lax.broadcasted_iota(jnp.int32, (SUB, LANES), 0)

    def fill(c, carry):
        ids = (slot + c * SUB).astype(jnp.float32)
        hits = [ids == splat_row(rank, t) for t in range(tiles)]
        target = []
        for k in range(6):
            found = jnp.zeros((SUB, LANES), jnp.float32)
            for t in range(tiles):
                found = found + jnp.where(hits[t], splat_row(own, 7 * t + k), 0.0)
            value = jnp.broadcast_to(jnp.sum(found, axis=1, keepdims=True), (SUB, LANES))
            targets[c, k] = value
            target.append(value)
        for k, value in enumerate(add_pairs(target, zeros6(), own)):
            sums[c, k] = value
        return carry

    lax.fori_loop(0, count[0], fill, 0)


def force_body(count, targets, running, *rest):
    sources, sums = rest[:-1], rest[-1]

    def chunk(c, carry):
        target = [targets[c, k] for k in range(6)]
        now = [running[c, k] for k in range(6)]
        for source in sources:
            now = add_pairs(target, now, source)
        for k in range(6):
            sums[c, k] = now[k]
        return carry

    lax.fori_loop(0, count[0], chunk, 0)


def final_body(scale, pieces, count, targets, running, rank, *rest):
    sources = rest[:pieces]
    pos, vel, acc, jerk, elapsed = rest[pieces : pieces + 5]
    new_pos, new_vel, new_acc, new_jerk = rest[pieces + 5 : pieces + 9]
    landed = rest[pieces + 9]
    tiles = pos.shape[1] // LANES
    slot = lax.broadcasted_iota(jnp.int32, (SUB, LANES), 0)
    landed[...] = jnp.zeros(landed.shape, jnp.float32)

    def chunk(c, carry):
        target = [targets[c, k] for k in range(6)]
        now = [running[c, k] for k in range(6)]
        for source in sources:
            now = add_pairs(target, now, source)
        ids = (slot + c * SUB).astype(jnp.float32)
        hits = [ids == splat_row(rank, t) for t in range(tiles)]
        for k in range(6):
            force = jnp.broadcast_to(jnp.sum(now[k], axis=1, keepdims=True), (SUB, LANES)) * scale
            for t in range(tiles):
                landed[t, k] += jnp.where(hits[t], force, 0.0)
        return carry

    lax.fori_loop(0, count[0], chunk, 0)
    for t in range(tiles):
        lanes = slice(t * LANES, (t + 1) * LANES)
        force = [jnp.sum(landed[t, k], axis=0, keepdims=True) for k in range(6)]
        acc_now = jnp.concatenate(force[0:3], axis=0)
        jerk_now = jnp.concatenate(force[3:6], axis=0)
        hit = jnp.broadcast_to(rank[t : t + 1, :], (3, LANES)) >= 0.0
        step = jnp.broadcast_to(elapsed[:, lanes], (3, LANES))
        half = 0.5 * step
        twelfth = step * step * (1.0 / 12.0)
        old_pos, old_vel = pos[:, lanes], vel[:, lanes]
        old_acc, old_jerk = acc[:, lanes], jerk[:, lanes]
        vel_now = old_vel + half * (old_acc + acc_now) + twelfth * (old_jerk - jerk_now)
        pos_now = old_pos + half * (old_vel + vel_now) + twelfth * (old_acc - acc_now)
        new_pos[:, lanes] = jnp.where(hit, pos_now, old_pos)
        new_vel[:, lanes] = jnp.where(hit, vel_now, old_vel)
        new_acc[:, lanes] = jnp.where(hit, acc_now, old_acc)
        new_jerk[:, lanes] = jnp.where(hit, jerk_now, old_jerk)


def partner(size, offset):
    if size & (size - 1) == 0:
        return [i ^ offset for i in range(size)]
    return [(i + offset) % size for i in range(size)]


def far_first(size):
    return list(range(size - 1, 0, -1))


def plan(plane, cores):
    pieces = [0] + far_first(plane)
    if cores == 1:
        return [("plane", k) for k in pieces[1:]]
    steps = [("core", 0)] + [("plane", k) for k in pieces[1:]]
    steps += [("core", k) for k in pieces[1:]]
    return steps


def on_device(positions, velocities, accels, jerks, masses, elapsed, active_star):
    f32 = jnp.float32
    stars = positions.shape[1]
    row_count = lax.axis_size("row")
    col_count = lax.axis_size("col")
    device_id = lax.axis_index("row") * col_count + lax.axis_index("col")
    scale = 1.0 / (stars * row_count * col_count)
    cores = 2 if row_count % 2 == 0 else 1
    plane = row_count // cores

    def send(value, move):
        pairs = []
        for r in range(row_count):
            for c in range(col_count):
                p, q, z = move(r // cores, r % cores, c)
                pairs.append((r * col_count + c, (p * cores + q) * col_count + z))
        return lax.ppermute(value, AXES, pairs)

    def along_col(value, k):
        to = partner(col_count, k)
        return send(value, lambda p, q, z: (p, q, to[z]))

    def along_plane(value, k):
        to = partner(plane, k)
        return send(value, lambda p, q, z: (to[p], q, z))

    def across(value):
        return send(value, lambda p, q, z: (p, 1 - q, z))

    wide = elapsed.reshape(1, stars)
    tiles = stars // LANES
    slots = -(-stars // SUB)
    own = pl.pallas_call(
        predict_body,
        out_shape=pltpu.VMEM((7 * tiles, LANES), f32),
        compiler_params=PARAMS,
        name="predict",
    )(*map(far, (positions, velocities, accels, jerks, masses.reshape(1, stars), wide)))
    line = [own] + [along_col(own, k) for k in far_first(col_count)]

    block = pltpu.VMEM((slots, 6, SUB, LANES), f32)
    count, rank, targets, sums = pl.pallas_call(
        setup_body,
        in_specs=[SMEM, VMEM, VMEM],
        out_shape=(
            pltpu.SMEM((1,), jnp.int32),
            pltpu.VMEM((max(SUB, tiles), LANES), f32),
            block,
            block,
        ),
        out_specs=(SMEM, VMEM, VMEM, VMEM),
        compiler_params=PARAMS,
        name="setup",
    )((device_id * stars).reshape(1).astype(jnp.int32), active_star.reshape(-1, LANES), near(own))

    def add_force(sums, *sources):
        return pl.pallas_call(
            force_body,
            in_specs=[SMEM] + [VMEM] * (2 + len(sources)),
            out_shape=block,
            out_specs=VMEM,
            input_output_aliases={2: 0},
            compiler_params=PARAMS,
            name="force",
        )(count, near(targets), near(sums), *map(near, sources))

    lined = jnp.concatenate(line, axis=0)
    pieces = {("plane", 0): lined}
    for k in far_first(plane):
        pieces["plane", k] = along_plane(lined, k)
    if cores == 2:
        for k in [0] + far_first(plane):
            pieces["core", k] = across(pieces["plane", k])
    sums = add_force(sums, *line[1:])
    steps = plan(plane, cores)
    for kind, k in steps[:-1]:
        sums = add_force(sums, pieces[kind, k])
    last = [pieces[step] for step in steps[-1:]]

    shape = jax.ShapeDtypeStruct(positions.shape, f32)
    return pl.pallas_call(
        functools.partial(final_body, scale, len(last)),
        in_specs=[SMEM] + [VMEM] * (3 + len(last) + 5),
        out_shape=(shape, shape, shape, shape),
        out_specs=(VMEM, VMEM, VMEM, VMEM),
        scratch_shapes=[pltpu.VMEM((tiles, 6, SUB, LANES), f32)],
        compiler_params=PARAMS,
        name="final",
    )(count, near(targets), near(sums), near(rank), *map(near, last), positions, velocities, accels, jerks, wide)


def solution(mesh):
    whole = P(None, AXES)

    return jax.shard_map(
        on_device,
        mesh=mesh,
        in_specs=(whole, whole, whole, whole, P(AXES), P(AXES), P()),
        out_specs=(whole, whole, whole, whole),
        check_vma=False,
    )
```

profile of v0, /device:TPU:1, one launch (start us, length us, event | category | flops | bytes accessed | tf_op | source)
XLA Modules:
  0.0 25.2 jit_solution(16014669154180532428)
XLA Ops:
  0.6 0.8 %predict.1.own = f32[28,128]{1,0:T(8,128)S(1)} custom-call(f32[3,512]{1,0:T(4,128)} %rest_1_.1, f32[3,512]{1,0:T(4,128)} %rest_2_.1, f32[3,512]{1,0:T(4,128)} %rest_3_.1, f32[3,512]{1,0:T(4,128)} %rest_4_.1, f32[1,512]{1,0:T(1,128)} %bitcast.7, f32[1,512]{1,0:T(1,128)} %bitcast.4), custom_call_target="tpu_custom_call" | custom-call | tf_op jit(solution)/shard_map/predict/pallas_call | solution.py:219
  1.4 4.2 %collective-permute-start = (f32[28,128]{1,0:T(8,128)S(1)}, f32[28,128]{1,0:T(8,128)S(1)}, u32[]{:S(2)}, u32[]{:S(2)}) collective-permute-start(f32[28,128]{1,0:T(8,128)S(1)} %predict.1.own), channel_id=1, source_target_pairs={{0,3},{1,2},{2,1},{3,0},{4,7},{5,6},{6,5},{7,4},{8,11},{9,10},{10,... | collective-permute-start | bytes 43016 | tf_op jit(solution)/shard_map/ppermute | solution.py:203
  5.6 0.0 collective-permute-start.1
  5.6 0.4 %collective-permute-start.2 = (f32[28,128]{1,0:T(8,128)S(1)}, f32[28,128]{1,0:T(8,128)S(1)}, u32[]{:S(2)}, u32[]{:S(2)}) collective-permute-start(f32[28,128]{1,0:T(8,128)S(1)} %predict.1.own), channel_id=1, source_target_pairs={{0,1},{1,0},{2,3},{3,2},{4,5},{5,4},{6,7},{7,6},{8,9},{9,8},{10,11... | collective-permute-start | bytes 43016 | tf_op jit(solution)/shard_map/ppermute | solution.py:203
  6.0 0.8 %collective-permute-done.rest_0_ = f32[28,128]{1,0:T(8,128)S(1)} collective-permute-done((f32[28,128]{1,0:T(8,128)S(1)}, f32[28,128]{1,0:T(8,128)S(1)}, u32[]{:S(2)}, u32[]{:S(2)}) %collective-permute-start) | collective-permute-done | bytes 14368 | tf_op jit(solution)/shard_map/ppermute | solution.py:203
  6.8 2.4 %collective-permute-done.1.rest_1_ = f32[28,128]{1,0:T(8,128)S(1)} collective-permute-done((f32[28,128]{1,0:T(8,128)S(1)}, f32[28,128]{1,0:T(8,128)S(1)}, u32[]{:S(2)}, u32[]{:S(2)}) %collective-permute-start.1) | collective-permute-done | bytes 14368 | tf_op jit(solution)/shard_map/ppermute | solution.py:203
  9.1 0.0 collective-permute-done.2.rest_2_
  9.1 2.2 %collective-permute-start.4 = (f32[112,128]{1,0:T(8,128)S(1)}, f32[112,128]{1,0:T(8,128)S(1)}, u32[]{:S(2)}, u32[]{:S(2)}) collective-permute-start(f32[112,128]{1,0:T(8,128)S(1)} %pad_maximum_fusion), channel_id=1, source_target_pairs={{0,24},{1,25},{2,26},{3,27},{4,28},{5,29},{6,30},{7,31},{8,16},{9,... | collective-permute-start | bytes 172040 | tf_op jit(solution)/shard_map/ppermute | solution.py:203
  11.4 0.2 collective-permute-start.5
  11.6 0.3 %collective-permute-start.6 = (f32[112,128]{1,0:T(8,128)S(1)}, f32[112,128]{1,0:T(8,128)S(1)}, u32[]{:S(2)}, u32[]{:S(2)}) collective-permute-start(f32[112,128]{1,0:T(8,128)S(1)} %pad_maximum_fusion), channel_id=1, source_target_pairs={{0,8},{1,9},{2,10},{3,11},{4,12},{5,13},{6,14},{7,15},{8,0},{9,1},... | collective-permute-start | bytes 172040 | tf_op jit(solution)/shard_map/ppermute | solution.py:203
  11.8 2.9 %collective-permute-start.3 = (f32[112,128]{1,0:T(8,128)S(1)}, f32[112,128]{1,0:T(8,128)S(1)}, u32[]{:S(2)}, u32[]{:S(2)}) collective-permute-start(f32[112,128]{1,0:T(8,128)S(1)} %pad_maximum_fusion), channel_id=1, source_target_pairs={{0,4},{1,5},{2,6},{3,7},{4,0},{5,1},{6,2},{7,3},{8,12},{9,13},{10,... | collective-permute-start | bytes 172040 | tf_op jit(solution)/shard_map/ppermute | solution.py:203
  14.8 0.0 collective-permute-done.4.rest_0_
  14.8 2.1 %collective-permute-start.7 = (f32[112,128]{1,0:T(8,128)S(1)}, f32[112,128]{1,0:T(8,128)S(1)}, u32[]{:S(2)}, u32[]{:S(2)}) collective-permute-start(f32[112,128]{1,0:T(8,128)S(1)} %collective-permute-done.4.rest_0_), channel_id=1, source_target_pairs={{0,4},{1,5},{2,6},{3,7},{4,0},{5,1},{6,2},{7,3},{8,12},{9,13},{10,... | collective-permute-start | bytes 172040 | tf_op jit(solution)/shard_map/ppermute | solution.py:203
  16.9 0.0 collective-permute-done.5.rest_0_
  16.9 1.0 %collective-permute-start.8 = (f32[112,128]{1,0:T(8,128)S(1)}, f32[112,128]{1,0:T(8,128)S(1)}, u32[]{:S(2)}, u32[]{:S(2)}) collective-permute-start(f32[112,128]{1,0:T(8,128)S(1)} %collective-permute-done.5.rest_0_), channel_id=1, source_target_pairs={{0,4},{1,5},{2,6},{3,7},{4,0},{5,1},{6,2},{7,3},{8,12},{9,13},{10,... | collective-permute-start | bytes 172040 | tf_op jit(solution)/shard_map/ppermute | solution.py:203
  17.9 0.0 collective-permute-done.6.rest_0_
  17.9 0.5 %collective-permute-start.9 = (f32[112,128]{1,0:T(8,128)S(1)}, f32[112,128]{1,0:T(8,128)S(1)}, u32[]{:S(2)}, u32[]{:S(2)}) collective-permute-start(f32[112,128]{1,0:T(8,128)S(1)} %collective-permute-done.6.rest_0_), channel_id=1, source_target_pairs={{0,4},{1,5},{2,6},{3,7},{4,0},{5,1},{6,2},{7,3},{8,12},{9,13},{10,... | collective-permute-start | bytes 172040 | tf_op jit(solution)/shard_map/ppermute | solution.py:203
  18.4 0.0 copy-start.5
  18.4 0.7 %copy-done.5 = s32[1024]{0:T(1024)S(1)} copy-done((s32[1024]{0:T(1024)S(1)}, s32[1024]{0:T(1024)}, u32[]{:S(2)}) %copy-start.5) | copy-done | bytes 4120
  19.1 0.9 %setup.1 = (s32[1]{0:T(128)S(4)}, f32[8,128]{1,0:T(8,128)S(1)}, f32[64,6,8,128]{3,2,1,0:T(8,128)S(1)}, f32[64,6,8,128]{3,2,1,0:T(8,128)S(1)}) custom-call(s32[1]{0:T(128)} %bitcast.base, s32[8,128]{1,0:T(8,128)S(1)} %bitcast.6, f32[28,128]{1,0:T(8,128)S(1)} %predict.1.own), custom_call_target="tpu_custom_call" | custom-call | tf_op jit(solution)/shard_map/setup/pallas_call | solution.py:228
  20.1 0.4 %force.7.running = f32[64,6,8,128]{3,2,1,0:T(8,128)S(1)} custom-call(s32[1]{0:T(128)S(4)} %get-tuple-element.8.count, f32[64,6,8,128]{3,2,1,0:T(8,128)S(1)} %get-tuple-element.9.targets, f32[64,6,8,128]{3,2,1,0:T(8,128)S(1)} %get-tuple-element.10.running, f32[28,128]{1,0:T(8,128)S(1)} %collective-permute-done.rest_0_, ...), custom_call_target="tpu_custom_call", output_to_operand_aliasing={{}: (2, {})} | custom-call | tf_op jit(solution)/shard_map/force/pallas_call | solution.py:243
  20.4 0.0 collective-permute-done.3.rest_0_
  20.4 0.5 %force.8.running = f32[64,6,8,128]{3,2,1,0:T(8,128)S(1)} custom-call(s32[1]{0:T(128)S(4)} %get-tuple-element.8.count, f32[64,6,8,128]{3,2,1,0:T(8,128)S(1)} %get-tuple-element.9.targets, f32[64,6,8,128]{3,2,1,0:T(8,128)S(1)} %force.7.running, f32[112,128]{1,0:T(8,128)S(1)} %collective-permute-done.3.rest_0_), custom_call_target="tpu_custom_call", output_to_operand_aliasing={{}: (2, {})} | custom-call | tf_op jit(solution)/shard_map/force/pallas_call | solution.py:243
  20.9 0.5 %force.9.running = f32[64,6,8,128]{3,2,1,0:T(8,128)S(1)} custom-call(s32[1]{0:T(128)S(4)} %get-tuple-element.8.count, f32[64,6,8,128]{3,2,1,0:T(8,128)S(1)} %get-tuple-element.9.targets, f32[64,6,8,128]{3,2,1,0:T(8,128)S(1)} %force.8.running, f32[112,128]{1,0:T(8,128)S(1)} %collective-permute-done.4.rest_0_), custom_call_target="tpu_custom_call", output_to_operand_aliasing={{}: (2, {})} | custom-call | tf_op jit(solution)/shard_map/force/pallas_call | solution.py:243
  21.4 0.5 %force.10.running = f32[64,6,8,128]{3,2,1,0:T(8,128)S(1)} custom-call(s32[1]{0:T(128)S(4)} %get-tuple-element.8.count, f32[64,6,8,128]{3,2,1,0:T(8,128)S(1)} %get-tuple-element.9.targets, f32[64,6,8,128]{3,2,1,0:T(8,128)S(1)} %force.9.running, f32[112,128]{1,0:T(8,128)S(1)} %collective-permute-done.5.rest_0_), custom_call_target="tpu_custom_call", output_to_operand_aliasing={{}: (2, {})} | custom-call | tf_op jit(solution)/shard_map/force/pallas_call | solution.py:243
  21.9 0.5 %force.11.running = f32[64,6,8,128]{3,2,1,0:T(8,128)S(1)} custom-call(s32[1]{0:T(128)S(4)} %get-tuple-element.8.count, f32[64,6,8,128]{3,2,1,0:T(8,128)S(1)} %get-tuple-element.9.targets, f32[64,6,8,128]{3,2,1,0:T(8,128)S(1)} %force.10.running, f32[112,128]{1,0:T(8,128)S(1)} %collective-permute-done.6.rest_0_), custom_call_target="tpu_custom_call", output_to_operand_aliasing={{}: (2, {})} | custom-call | tf_op jit(solution)/shard_map/force/pallas_call | solution.py:243
  22.4 0.0 collective-permute-done.7.rest_0_
  22.4 0.5 %force.12.running = f32[64,6,8,128]{3,2,1,0:T(8,128)S(1)} custom-call(s32[1]{0:T(128)S(4)} %get-tuple-element.8.count, f32[64,6,8,128]{3,2,1,0:T(8,128)S(1)} %get-tuple-element.9.targets, f32[64,6,8,128]{3,2,1,0:T(8,128)S(1)} %force.11.running, f32[112,128]{1,0:T(8,128)S(1)} %collective-permute-done.7.rest_0_), custom_call_target="tpu_custom_call", output_to_operand_aliasing={{}: (2, {})} | custom-call | tf_op jit(solution)/shard_map/force/pallas_call | solution.py:243
  22.9 0.0 copy-start
  22.9 0.0 copy-start.1
  22.9 0.0 copy-start.2
  22.9 0.0 copy-start.3
  22.9 0.0 copy-start.4
  22.9 0.0 collective-permute-done.8.rest_0_
  23.0 0.5 %force.13.running = f32[64,6,8,128]{3,2,1,0:T(8,128)S(1)} custom-call(s32[1]{0:T(128)S(4)} %get-tuple-element.8.count, f32[64,6,8,128]{3,2,1,0:T(8,128)S(1)} %get-tuple-element.9.targets, f32[64,6,8,128]{3,2,1,0:T(8,128)S(1)} %force.12.running, f32[112,128]{1,0:T(8,128)S(1)} %collective-permute-done.8.rest_0_), custom_call_target="tpu_custom_call", output_to_operand_aliasing={{}: (2, {})} | custom-call | tf_op jit(solution)/shard_map/force/pallas_call | solution.py:243
  23.4 0.0 collective-permute-done.9.rest_0_
  23.5 0.1 copy-done
  23.6 0.0 copy-done.1
  23.6 0.0 copy-done.2
  23.6 0.0 copy-done.3
  23.6 0.0 copy-done.4
  23.6 1.5 %final.1 = (f32[3,512]{1,0:T(4,128)}, f32[3,512]{1,0:T(4,128)}, f32[3,512]{1,0:T(4,128)}, f32[3,512]{1,0:T(4,128)}) custom-call(s32[1]{0:T(128)S(4)} %get-tuple-element.8.count, f32[64,6,8,128]{3,2,1,0:T(8,128)S(1)} %get-tuple-element.9.targets, f32[64,6,8,128]{3,2,1,0:T(8,128)S(1)} %force.13.running, f32[8,128]{1,0:T(8,128)S(1)} %get-tuple-element.11.rank, ...), custom_call_target="tpu_custom_call" | custom-call | tf_op jit(solution)/shard_map/final/pallas_call | solution.py:267
  (1 shorter events, 0.0 us)
Async XLA Ops:
  1.4 5.3 %collective-permute-start = (f32[28,128]{1,0:T(8,128)S(1)}, f32[28,128]{1,0:T(8,128)S(1)}, u32[]{:S(2)}, u32[]{:S(2)}) collective-permute-start(f32[28,128]{1,0:T(8,128)S(1)} %predict.1.own), channel_id=1, source_target_pairs={{0,3},{1,2},{2,1},{3,0},{4,7},{5,6},{6,5},{7,4},{8,11},{9,10},{10,... | collective-permute-start | bytes 43016 | tf_op jit(solution)/shard_map/ppermute | solution.py:203
  5.6 3.5 %collective-permute-start.1 = (f32[28,128]{1,0:T(8,128)S(1)}, f32[28,128]{1,0:T(8,128)S(1)}, u32[]{:S(2)}, u32[]{:S(2)}) collective-permute-start(f32[28,128]{1,0:T(8,128)S(1)} %predict.1.own), channel_id=1, source_target_pairs={{0,2},{1,3},{2,0},{3,1},{4,6},{5,7},{6,4},{7,5},{8,10},{9,11},{10,... | collective-permute-start | bytes 43016 | tf_op jit(solution)/shard_map/ppermute | solution.py:203
  5.6 3.5 %collective-permute-start.2 = (f32[28,128]{1,0:T(8,128)S(1)}, f32[28,128]{1,0:T(8,128)S(1)}, u32[]{:S(2)}, u32[]{:S(2)}) collective-permute-start(f32[28,128]{1,0:T(8,128)S(1)} %predict.1.own), channel_id=1, source_target_pairs={{0,1},{1,0},{2,3},{3,2},{4,5},{5,4},{6,7},{7,6},{8,9},{9,8},{10,11... | collective-permute-start | bytes 43016 | tf_op jit(solution)/shard_map/ppermute | solution.py:203
  9.1 5.7 %collective-permute-start.4 = (f32[112,128]{1,0:T(8,128)S(1)}, f32[112,128]{1,0:T(8,128)S(1)}, u32[]{:S(2)}, u32[]{:S(2)}) collective-permute-start(f32[112,128]{1,0:T(8,128)S(1)} %pad_maximum_fusion), channel_id=1, source_target_pairs={{0,24},{1,25},{2,26},{3,27},{4,28},{5,29},{6,30},{7,31},{8,16},{9,... | collective-permute-start | bytes 172040 | tf_op jit(solution)/shard_map/ppermute | solution.py:203
  11.4 5.5 %collective-permute-start.5 = (f32[112,128]{1,0:T(8,128)S(1)}, f32[112,128]{1,0:T(8,128)S(1)}, u32[]{:S(2)}, u32[]{:S(2)}) collective-permute-start(f32[112,128]{1,0:T(8,128)S(1)} %pad_maximum_fusion), channel_id=1, source_target_pairs={{0,16},{1,17},{2,18},{3,19},{4,20},{5,21},{6,22},{7,23},{8,24},{9,... | collective-permute-start | bytes 172040 | tf_op jit(solution)/shard_map/ppermute | solution.py:203
  11.6 6.3 %collective-permute-start.6 = (f32[112,128]{1,0:T(8,128)S(1)}, f32[112,128]{1,0:T(8,128)S(1)}, u32[]{:S(2)}, u32[]{:S(2)}) collective-permute-start(f32[112,128]{1,0:T(8,128)S(1)} %pad_maximum_fusion), channel_id=1, source_target_pairs={{0,8},{1,9},{2,10},{3,11},{4,12},{5,13},{6,14},{7,15},{8,0},{9,1},... | collective-permute-start | bytes 172040 | tf_op jit(solution)/shard_map/ppermute | solution.py:203
  11.8 8.6 %collective-permute-start.3 = (f32[112,128]{1,0:T(8,128)S(1)}, f32[112,128]{1,0:T(8,128)S(1)}, u32[]{:S(2)}, u32[]{:S(2)}) collective-permute-start(f32[112,128]{1,0:T(8,128)S(1)} %pad_maximum_fusion), channel_id=1, source_target_pairs={{0,4},{1,5},{2,6},{3,7},{4,0},{5,1},{6,2},{7,3},{8,12},{9,13},{10,... | collective-permute-start | bytes 172040 | tf_op jit(solution)/shard_map/ppermute | solution.py:203
  14.8 7.6 %collective-permute-start.7 = (f32[112,128]{1,0:T(8,128)S(1)}, f32[112,128]{1,0:T(8,128)S(1)}, u32[]{:S(2)}, u32[]{:S(2)}) collective-permute-start(f32[112,128]{1,0:T(8,128)S(1)} %collective-permute-done.4.rest_0_), channel_id=1, source_target_pairs={{0,4},{1,5},{2,6},{3,7},{4,0},{5,1},{6,2},{7,3},{8,12},{9,13},{10,... | collective-permute-start | bytes 172040 | tf_op jit(solution)/shard_map/ppermute | solution.py:203
  16.9 6.1 %collective-permute-start.8 = (f32[112,128]{1,0:T(8,128)S(1)}, f32[112,128]{1,0:T(8,128)S(1)}, u32[]{:S(2)}, u32[]{:S(2)}) collective-permute-start(f32[112,128]{1,0:T(8,128)S(1)} %collective-permute-done.5.rest_0_), channel_id=1, source_target_pairs={{0,4},{1,5},{2,6},{3,7},{4,0},{5,1},{6,2},{7,3},{8,12},{9,13},{10,... | collective-permute-start | bytes 172040 | tf_op jit(solution)/shard_map/ppermute | solution.py:203
  17.9 5.5 %collective-permute-start.9 = (f32[112,128]{1,0:T(8,128)S(1)}, f32[112,128]{1,0:T(8,128)S(1)}, u32[]{:S(2)}, u32[]{:S(2)}) collective-permute-start(f32[112,128]{1,0:T(8,128)S(1)} %collective-permute-done.6.rest_0_), channel_id=1, source_target_pairs={{0,4},{1,5},{2,6},{3,7},{4,0},{5,1},{6,2},{7,3},{8,12},{9,13},{10,... | collective-permute-start | bytes 172040 | tf_op jit(solution)/shard_map/ppermute | solution.py:203
  18.4 0.7 %copy-start.5 = (s32[1024]{0:T(1024)S(1)}, s32[1024]{0:T(1024)}, u32[]{:S(2)}) copy-start(s32[1024]{0:T(1024)} %param.13) | copy-start | bytes 12292
  22.9 0.7 %copy-start = (f32[3,512]{1,0:T(4,128)S(1)}, f32[3,512]{1,0:T(4,128)}, u32[]{:S(2)}) copy-start(f32[3,512]{1,0:T(4,128)} %rest_1_.1) | copy-start | bytes 18436
  22.9 0.7 %copy-start.1 = (f32[3,512]{1,0:T(4,128)S(1)}, f32[3,512]{1,0:T(4,128)}, u32[]{:S(2)}) copy-start(f32[3,512]{1,0:T(4,128)} %rest_2_.1) | copy-start | bytes 18436
  22.9 0.7 %copy-start.2 = (f32[3,512]{1,0:T(4,128)S(1)}, f32[3,512]{1,0:T(4,128)}, u32[]{:S(2)}) copy-start(f32[3,512]{1,0:T(4,128)} %rest_3_.1) | copy-start | bytes 18436
  22.9 0.7 %copy-start.3 = (f32[3,512]{1,0:T(4,128)S(1)}, f32[3,512]{1,0:T(4,128)}, u32[]{:S(2)}) copy-start(f32[3,512]{1,0:T(4,128)} %rest_4_.1) | copy-start | bytes 18436
  22.9 0.7 %copy-start.4 = (f32[512]{0:T(512)S(1)}, f32[512]{0:T(512)}, u32[]{:S(2)}) copy-start(f32[512]{0:T(512)} %param.12) | copy-start | bytes 6148
where the time goes:
time: 25.5 us; the launch traced here: 25.2 us
  starting transfers between devices  13.9 us (55%)
  Pallas kernels  6.52 us (26%)
  waiting for transfers between devices  3.15 us (12%)
  local copies, waits for them, and re-layouts  0.89 us (3%)
  between operations  0.76 us (3%)
    ppermute x10, starting transfers between devices, send(): return lax.ppermute(value, AXES, pairs)  13.9 us
    pallas_call x7, Pallas kernels, add_force(): pl.pallas_call(force_body, in_specs=[SMEM] + [VMEM] * (2 + len(sources)),...  3.27 us
    ppermute x10, waiting for transfers between devices, send(): return lax.ppermute(value, AXES, pairs)  3.15 us
    pallas_call x1, Pallas kernels, on_device(): pl.pallas_call(functools.partial(final_body, scale, len(last)), in_specs=...  1.54 us
    pallas_call x1, Pallas kernels, on_device(): pl.pallas_call(setup_body, in_specs=[SMEM, VMEM, VMEM], out_shape=(pltpu....  0.92 us
    unnamed x12, local copies, waits for them, and re-layouts  0.89 us
    pallas_call x1, Pallas kernels, on_device(): pl.pallas_call(predict_body, out_shape=pltpu.VMEM((7 * tiles, LANES), f32...  0.79 us
  transfers between devices with their start and end apart: 10, of which 2 were waited for; matrix products, arithmetic and copies ran while one was open for 0% of the time, Pallas kernels for 17%

commit v1 on v0

v1 whole, which is shorter than its diff:
```python
import functools

import jax
import jax.numpy as jnp
from jax import lax
from jax.experimental import pallas as pl
from jax.experimental.pallas import tpu as pltpu
from jax.sharding import PartitionSpec as P


softening = 0.001
LANES = 128
SUB = 8
GROUP = 4
AXES = ("row", "col")
VMEM = pl.BlockSpec(memory_space=pltpu.VMEM)
SMEM = pl.BlockSpec(memory_space=pltpu.SMEM)


PARAMS = pltpu.CompilerParams(vmem_limit_bytes=4 << 20)


def near(value):
    return pltpu.with_memory_space_constraint(value, pltpu.VMEM)


def far(value):
    return pltpu.with_memory_space_constraint(value, pltpu.HBM)


def predict_body(pos, vel, acc, jerk, mass, elapsed, active, out, *kept):
    for source, copy in zip((pos, vel, acc, jerk, elapsed, active), kept):
        copy[...] = source[...]
    step = elapsed[...]
    moved_pos = pos[...] + step * (vel[...] + step * (0.5 * acc[...] + step * jerk[...] * (1.0 / 6.0)))
    moved_vel = vel[...] + step * (acc[...] + 0.5 * step * jerk[...])
    for tile in range(pos.shape[1] // LANES):
        lanes = slice(tile * LANES, (tile + 1) * LANES)
        out[7 * tile : 7 * tile + 3, :] = moved_pos[:, lanes]
        out[7 * tile + 3 : 7 * tile + 6, :] = moved_vel[:, lanes]
        out[7 * tile + 6 : 7 * tile + 7, :] = mass[:, lanes]


def splat_row(ref, row):
    return jnp.broadcast_to(ref[row : row + 1, :], (SUB, LANES))


def add_pairs(target, sums, source, first=0):
    sums = list(sums)
    for base in range(first, source.shape[0], 7):
        sep = [splat_row(source, base + k) - target[k] for k in range(3)]
        rel = [splat_row(source, base + 3 + k) - target[3 + k] for k in range(3)]
        radius_sq = (sep[0] * sep[0] + sep[1] * sep[1]) + (sep[2] * sep[2] + softening)
        inverse = lax.rsqrt(radius_sq)
        inverse_sq = inverse * inverse
        weight = (splat_row(source, base + 6) * inverse) * inverse_sq
        dot = (sep[0] * rel[0] + sep[1] * rel[1]) + sep[2] * rel[2]
        closing = (3.0 * inverse_sq) * dot
        for k in range(3):
            sums[k] = sums[k] + weight * sep[k]
            sums[3 + k] = sums[3 + k] + weight * (rel[k] - closing * sep[k])
    return sums


def zeros6():
    return [jnp.zeros((SUB, LANES), jnp.float32) for _ in range(6)]


def setup_body(base, active, own, near_by, count, rank, targets, sums):
    tiles = own.shape[0] // 7
    rows = max(SUB, tiles)
    sub_rows = lax.broadcasted_iota(jnp.int32, (rows, LANES), 0)
    sub_lanes = lax.broadcasted_iota(jnp.int32, (LANES, LANES), 0)
    lane_cols = lax.broadcasted_iota(jnp.int32, (LANES, LANES), 1)
    flags = jnp.zeros((rows, LANES), jnp.float32)
    for r in range(active.shape[0]):
        local = active[r : r + 1, :] - base[0]
        high = local >> 7
        high = jnp.where(high < tiles, high, -1)
        low = local & 127
        one = (sub_rows == high).astype(jnp.float32)
        two = (sub_lanes == low).astype(jnp.float32)
        flags = flags + lax.dot_general(
            one, two, (((1,), (1,)), ((), ())), preferred_element_type=jnp.float32
        )
    before = (sub_lanes < lane_cols).astype(jnp.float32)
    order = jnp.dot(flags, before, preferred_element_type=jnp.float32)
    in_row = jnp.sum(flags, axis=1, keepdims=True)
    for r in range(tiles - 1):
        order = order + jnp.where(sub_rows > r, in_row[r : r + 1, :], 0.0)
    rank[...] = jnp.where(flags > 0.5, order, -1.0)
    total = jnp.sum(flags).astype(jnp.int32)
    count[0] = (total + (SUB - 1)) // SUB
    slot = lax.broadcasted_iota(jnp.int32, (SUB, LANES), 0)
    lane = lax.broadcasted_iota(jnp.int32, (SUB, LANES), 1)

    def fill(c, carry):
        ids = (slot + c * SUB).astype(jnp.float32)
        hits = [ids == splat_row(rank, t) for t in range(tiles)]
        target = []
        packed = jnp.zeros((SUB, LANES), jnp.float32)
        for k in range(6):
            found = jnp.zeros((SUB, LANES), jnp.float32)
            for t in range(tiles):
                found = found + jnp.where(hits[t], splat_row(own, 7 * t + k), 0.0)
            value = jnp.broadcast_to(jnp.sum(found, axis=1, keepdims=True), (SUB, LANES))
            packed = jnp.where(lane == k, value, packed)
            target.append(value)
        targets[c] = packed
        for k, value in enumerate(add_pairs(target, zeros6(), near_by)):
            sums[c, k] = value
        return carry

    lax.fori_loop(0, count[0], fill, 0)


def add_piece(first, lead, count, targets, running, sent, got, sums):
    def unpack(c):
        packed = targets[c]
        return tuple(jnp.broadcast_to(packed[:, k : k + 1], (SUB, LANES)) for k in range(6))

    def add_from(source):
        def chunk(c, target):
            following = unpack(c + 1)
            now = add_pairs(target, [running[c, k] for k in range(6)], source, first)
            for k in range(6):
                sums[c, k] = now[k]
            return following

        lax.fori_loop(0, count[0], chunk, unpack(0))

    if got is None:
        add_from(sent)
        return

    @pl.when(lead[0] == 1)
    def from_link():
        add_from(sent)

    @pl.when(lead[0] != 1)
    def from_core():
        add_from(got)


def force_body(first, shared, lead, count, targets, running, *rest):
    sent, got, sums = (rest[0], rest[1], rest[2]) if shared else (rest[0], None, rest[1])
    add_piece(first, lead, count, targets, running, sent, got, sums)


def final_body(first, shared, scale, lead, count, targets, running, *rest):
    sent, got, rest = (rest[0], rest[1], rest[2:]) if shared else (rest[0], None, rest[1:])
    rank, pos, vel, acc, jerk, elapsed, new_pos, new_vel, new_acc, new_jerk, sums, landed = rest
    tiles = pos.shape[1] // LANES
    add_piece(first, lead, count, targets, running, sent, got, sums)
    slot = lax.broadcasted_iota(jnp.int32, (SUB, LANES), 0)
    landed[...] = jnp.zeros(landed.shape, jnp.float32)

    def land(g, carry):
        for c in range(GROUP):
            chunk = g * GROUP + c
            ids = (slot + chunk * SUB).astype(jnp.float32)
            hits = [ids == splat_row(rank, t) for t in range(tiles)]
            for k in range(6):
                total = jnp.sum(sums[chunk, k], axis=1, keepdims=True)
                force = jnp.broadcast_to(total, (SUB, LANES)) * scale
                for t in range(tiles):
                    landed[t, k] += jnp.where(hits[t], force, 0.0)
        return carry

    lax.fori_loop(0, (count[0] + (GROUP - 1)) // GROUP, land, 0)
    for t in range(tiles):
        lanes = slice(t * LANES, (t + 1) * LANES)
        force = [jnp.sum(landed[t, k], axis=0, keepdims=True) for k in range(6)]
        acc_now = jnp.concatenate(force[0:3], axis=0)
        jerk_now = jnp.concatenate(force[3:6], axis=0)
        hit = jnp.broadcast_to(rank[t : t + 1, :], (3, LANES)) >= 0.0
        step = jnp.broadcast_to(elapsed[:, lanes], (3, LANES))
        half = 0.5 * step
        twelfth = step * step * (1.0 / 12.0)
        old_pos, old_vel = pos[:, lanes], vel[:, lanes]
        old_acc, old_jerk = acc[:, lanes], jerk[:, lanes]
        vel_now = old_vel + half * (old_acc + acc_now) + twelfth * (old_jerk - jerk_now)
        pos_now = old_pos + half * (old_vel + vel_now) + twelfth * (old_acc - acc_now)
        new_pos[:, lanes] = jnp.where(hit, pos_now, old_pos)
        new_vel[:, lanes] = jnp.where(hit, vel_now, old_vel)
        new_acc[:, lanes] = jnp.where(hit, acc_now, old_acc)
        new_jerk[:, lanes] = jnp.where(hit, jerk_now, old_jerk)


def partner(size, offset):
    if size & (size - 1) == 0:
        return [i ^ offset for i in range(size)]
    return [(i + offset) % size for i in range(size)]


def sizes(mesh_shape):
    row_count, col_count = mesh_shape
    cores = 2 if row_count % 2 == 0 else 1
    return cores, row_count // cores, col_count


def col_order(count):
    middle = count // 2
    return ([middle] if middle > 1 else []) + [k for k in range(count - 1, 0, -1) if k != middle or k == 1]


def on_device(positions, velocities, accels, jerks, masses, elapsed, active_star):
    f32, i32 = jnp.float32, jnp.int32
    stars = positions.shape[1]
    row_count = lax.axis_size("row")
    col_count = lax.axis_size("col")
    row_index = lax.axis_index("row")
    device_id = row_index * col_count + lax.axis_index("col")
    scale = 1.0 / (stars * row_count * col_count)
    cores, plane, _ = sizes((row_count, col_count))

    def send(value, move):
        pairs = []
        for r in range(row_count):
            for c in range(col_count):
                p, q, z = move(r // cores, r % cores, c)
                pairs.append((r * col_count + c, (p * cores + q) * col_count + z))
        return lax.ppermute(value, AXES, pairs)

    def along_col(value, k):
        to = partner(col_count, k)
        idle = partner(plane, 1) if plane > 1 else None

        def move(p, q, z):
            if q == cores - 1 or idle is None:
                return p, q, to[z]
            return idle[p], q, z

        return send(value, move)

    def along_plane(value, k):
        to = partner(plane, k)
        idle = partner(col_count, 1) if col_count > 1 else None

        def move(p, q, z):
            if q == cores - 1 or idle is None:
                return to[p], q, z
            return p, q, idle[z]

        return send(value, move)

    def across(value):
        return send(value, lambda p, q, z: (p, 1 - q, z))

    wide = elapsed.reshape(1, stars)
    active = active_star.reshape(-1, LANES)
    tiles = stars // LANES
    slots = -(-stars // SUB)
    state = (positions, velocities, accels, jerks)
    own, *kept, wide, active = pl.pallas_call(
        predict_body,
        out_shape=(
            pltpu.VMEM((7 * tiles, LANES), f32),
            *(pltpu.VMEM(x.shape, f32) for x in state),
            pltpu.VMEM(wide.shape, f32),
            pltpu.VMEM(active.shape, i32),
        ),
        compiler_params=PARAMS,
        name="predict",
    )(*map(far, (*state, masses.reshape(1, stars), wide, active)))

    chip = jnp.concatenate([own, across(own)], axis=0) if cores == 2 else own
    found = [along_col(chip, k) for k in col_order(col_count)]

    block = pltpu.VMEM((slots, 6, SUB, LANES), f32)
    count, rank, targets, sums = pl.pallas_call(
        setup_body,
        in_specs=[SMEM, VMEM, VMEM, VMEM],
        out_shape=(
            pltpu.SMEM((1,), i32),
            pltpu.VMEM((max(SUB, tiles), LANES), f32),
            pltpu.VMEM((slots + 1, SUB, LANES), f32),
            block,
        ),
        out_specs=(SMEM, VMEM, VMEM, VMEM),
        compiler_params=PARAMS,
        name="setup",
    )((device_id * stars).reshape(1).astype(i32), near(active), near(own), near(chip))

    line = jnp.concatenate([chip, *found], axis=0)
    pieces = [("line", line, chip.shape[0])]
    pieces += [(f"plane_{k}", along_plane(line, k), 0) for k in range(1, plane)]
    shared = cores == 2
    lead = (row_index % cores == cores - 1).reshape(1).astype(i32)
    held = []
    for name, value, first in pieces:
        both = [value, across(value)] if shared else [value]
        held.append((name, first, both))
    for name, first, both in held[:-1]:
        sums = pl.pallas_call(
            functools.partial(force_body, first, shared),
            in_specs=[SMEM, SMEM] + [VMEM] * (2 + len(both)),
            out_shape=block,
            out_specs=VMEM,
            input_output_aliases={3: 0},
            compiler_params=PARAMS,
            name="force",
        )(lead, count, near(targets), near(sums), *map(near, both))

    name, first, both = held[-1]
    shape = jax.ShapeDtypeStruct(positions.shape, f32)
    near_args = (targets, sums, *both, rank, *kept, wide)
    return pl.pallas_call(
        functools.partial(final_body, first, shared, scale),
        in_specs=[SMEM, SMEM] + [VMEM] * len(near_args),
        out_shape=(shape, shape, shape, shape),
        out_specs=(VMEM, VMEM, VMEM, VMEM),
        scratch_shapes=[
            pltpu.VMEM((slots + GROUP, 6, SUB, LANES), f32),
            pltpu.VMEM((tiles, 6, SUB, LANES), f32),
        ],
        compiler_params=PARAMS,
        name="final",
    )(lead, count, *map(near, near_args))


def solution(mesh):
    whole = P(None, AXES)

    return jax.shard_map(
        on_device,
        mesh=mesh,
        in_specs=(whole, whole, whole, whole, P(AXES), P(AXES), P()),
        out_specs=(whole, whole, whole, whole),
        check_vma=False,
    )
```

time: 25.5 us -> 23.9 us (0.937)
  the two profiles are of different devices: /device:TPU:1 before, /device:TPU:18 now
where the time goes in v1:
time: 23.9 us; the launch traced here: 23.7 us
  waiting for transfers between devices  8.5 us (36%)
  Pallas kernels  8.07 us (34%)
  starting transfers between devices  6.37 us (27%)
  between operations  0.72 us (3%)
    ppermute x11, waiting for transfers between devices, send(): return lax.ppermute(value, AXES, pairs)  8.5 us
    ppermute x11, starting transfers between devices, send(): return lax.ppermute(value, AXES, pairs)  6.37 us
    pallas_call x3, Pallas kernels, on_device(): pl.pallas_call(functools.partial(force_body, first, shared), in_specs=[SM...  3.74 us
    pallas_call x1, Pallas kernels, on_device(): pl.pallas_call(functools.partial(final_body, first, shared, scale), in_sp...  2.22 us
    pallas_call x1, Pallas kernels, on_device(): pl.pallas_call(setup_body, in_specs=[SMEM, VMEM, VMEM, VMEM], out_shape=(...  1.3 us
    pallas_call x1, Pallas kernels, on_device(): pl.pallas_call(predict_body, out_shape=(pltpu.VMEM((7 * tiles, LANES), f3...  0.81 us
  transfers between devices with their start and end apart: 11, of which 7 were waited for; matrix products, arithmetic and copies ran while one was open for 0% of the time, Pallas kernels for 21%

profile of v1, /device:TPU:18, one launch (start us, length us, event | category | flops | bytes accessed | tf_op | source)
XLA Modules:
  0.0 23.7 jit_solution(6147404910569835579)
XLA Ops:
  0.6 0.8 %predict.1 = (f32[28,128]{1,0:T(8,128)S(1)}, f32[3,512]{1,0:T(4,128)S(1)}, f32[3,512]{1,0:T(4,128)S(1)}, f32[3,512]{1,0:T(4,128)S(1)}, f32[3,512]{1,0:T(4,128)S(...) custom-call(f32[3,512]{1,0:T(4,128)} %pos.1, f32[3,512]{1,0:T(4,128)} %vel.1, f32[3,512]{1,0:T(4,128)} %acc.1, ...), custom_call_target="tpu_custom_call" | custom-call | tf_op jit(solution)/shard_map/predict/pallas_call | solution.py:255
  1.4 0.1 collective-permute-start
  1.5 1.2 %collective-permute-done = f32[28,128]{1,0:T(8,128)S(1)} collective-permute-done((f32[28,128]{1,0:T(8,128)S(1)}, f32[28,128]{1,0:T(8,128)S(1)}, u32[]{:S(2)}, u32[]{:S(2)}) %collective-permute-start) | collective-permute-done | bytes 14368 | tf_op jit(solution)/shard_map/ppermute | solution.py:223
  2.7 0.6 %collective-permute-start.1 = (f32[56,128]{1,0:T(8,128)S(1)}, f32[56,128]{1,0:T(8,128)S(1)}, u32[]{:S(2)}, u32[]{:S(2)}) collective-permute-start(f32[56,128]{1,0:T(8,128)S(1)} %pad_maximum_fusion.near_by), channel_id=1, source_target_pairs={{0,8},{1,9},{2,10},{3,11},{4,6},{5,7},{6,4},{7,5},{8,0},{9,1},{10,... | collective-permute-start | bytes 86024 | tf_op jit(solution)/shard_map/ppermute | solution.py:223
  3.3 1.5 %collective-permute-start.2 = (f32[56,128]{1,0:T(8,128)S(1)}, f32[56,128]{1,0:T(8,128)S(1)}, u32[]{:S(2)}, u32[]{:S(2)}) collective-permute-start(f32[56,128]{1,0:T(8,128)S(1)} %pad_maximum_fusion.near_by), channel_id=1, source_target_pairs={{0,8},{1,9},{2,10},{3,11},{4,7},{5,6},{6,5},{7,4},{8,0},{9,1},{10,... | collective-permute-start | bytes 86024 | tf_op jit(solution)/shard_map/ppermute | solution.py:223
  4.8 0.5 %collective-permute-start.3 = (f32[56,128]{1,0:T(8,128)S(1)}, f32[56,128]{1,0:T(8,128)S(1)}, u32[]{:S(2)}, u32[]{:S(2)}) collective-permute-start(f32[56,128]{1,0:T(8,128)S(1)} %pad_maximum_fusion.near_by), channel_id=1, source_target_pairs={{0,8},{1,9},{2,10},{3,11},{4,5},{5,4},{6,7},{7,6},{8,0},{9,1},{10,... | collective-permute-start | bytes 86024 | tf_op jit(solution)/shard_map/ppermute | solution.py:223
  5.3 1.3 %collective-permute-done.1 = f32[56,128]{1,0:T(8,128)S(1)} collective-permute-done((f32[56,128]{1,0:T(8,128)S(1)}, f32[56,128]{1,0:T(8,128)S(1)}, u32[]{:S(2)}, u32[]{:S(2)}) %collective-permute-start.1) | collective-permute-done | bytes 28704 | tf_op jit(solution)/shard_map/ppermute | solution.py:223
  6.6 0.5 %collective-permute-done.2 = f32[56,128]{1,0:T(8,128)S(1)} collective-permute-done((f32[56,128]{1,0:T(8,128)S(1)}, f32[56,128]{1,0:T(8,128)S(1)}, u32[]{:S(2)}, u32[]{:S(2)}) %collective-permute-start.2) | collective-permute-done | bytes 28704 | tf_op jit(solution)/shard_map/ppermute | solution.py:223
  7.2 1.5 %collective-permute-done.3 = f32[56,128]{1,0:T(8,128)S(1)} collective-permute-done((f32[56,128]{1,0:T(8,128)S(1)}, f32[56,128]{1,0:T(8,128)S(1)}, u32[]{:S(2)}, u32[]{:S(2)}) %collective-permute-start.3) | collective-permute-done | bytes 28704 | tf_op jit(solution)/shard_map/ppermute | solution.py:223
  8.7 0.1 concatenate.8.rest_0_
  8.7 1.6 %collective-permute-start.5 = (f32[224,128]{1,0:T(8,128)S(1)}, f32[224,128]{1,0:T(8,128)S(1)}, u32[]{:S(2)}, u32[]{:S(2)}) collective-permute-start(f32[224,128]{1,0:T(8,128)S(1)} %concatenate.8.rest_0_), channel_id=1, source_target_pairs={{0,1},{1,0},{2,3},{3,2},{4,12},{5,13},{6,14},{7,15},{8,9},{9,8},{1... | collective-permute-start | bytes 344072 | tf_op jit(solution)/shard_map/ppermute | solution.py:223
  10.4 0.4 %collective-permute-start.7 = (f32[224,128]{1,0:T(8,128)S(1)}, f32[224,128]{1,0:T(8,128)S(1)}, u32[]{:S(2)}, u32[]{:S(2)}) collective-permute-start(f32[224,128]{1,0:T(8,128)S(1)} %concatenate.8.rest_0_), channel_id=1, source_target_pairs={{0,1},{1,0},{2,3},{3,2},{4,20},{5,21},{6,22},{7,23},{8,9},{9,8},{1... | collective-permute-start | bytes 344072 | tf_op jit(solution)/shard_map/ppermute | solution.py:223
  10.8 1.6 %collective-permute-start.9 = (f32[224,128]{1,0:T(8,128)S(1)}, f32[224,128]{1,0:T(8,128)S(1)}, u32[]{:S(2)}, u32[]{:S(2)}) collective-permute-start(f32[224,128]{1,0:T(8,128)S(1)} %concatenate.8.rest_0_), channel_id=1, source_target_pairs={{0,1},{1,0},{2,3},{3,2},{4,28},{5,29},{6,30},{7,31},{8,9},{9,8},{1... | collective-permute-start | bytes 344072 | tf_op jit(solution)/shard_map/ppermute | solution.py:223
  12.4 0.0 collective-permute-start.4
  12.4 1.2 %collective-permute-done.5.rest_0_ = f32[224,128]{1,0:T(8,128)S(1)} collective-permute-done((f32[224,128]{1,0:T(8,128)S(1)}, f32[224,128]{1,0:T(8,128)S(1)}, u32[]{:S(2)}, u32[]{:S(2)}) %collective-permute-start.5) | collective-permute-done | bytes 114720 | tf_op jit(solution)/shard_map/ppermute | solution.py:223
  13.6 0.0 collective-permute-start.6
  13.6 1.6 %collective-permute-done.7.rest_0_ = f32[224,128]{1,0:T(8,128)S(1)} collective-permute-done((f32[224,128]{1,0:T(8,128)S(1)}, f32[224,128]{1,0:T(8,128)S(1)}, u32[]{:S(2)}, u32[]{:S(2)}) %collective-permute-start.7) | collective-permute-done | bytes 114720 | tf_op jit(solution)/shard_map/ppermute | solution.py:223
  15.2 0.0 collective-permute-start.8
  15.2 1.2 %collective-permute-done.9.rest_0_ = f32[224,128]{1,0:T(8,128)S(1)} collective-permute-done((f32[224,128]{1,0:T(8,128)S(1)}, f32[224,128]{1,0:T(8,128)S(1)}, u32[]{:S(2)}, u32[]{:S(2)}) %collective-permute-start.9) | collective-permute-done | bytes 114720 | tf_op jit(solution)/shard_map/ppermute | solution.py:223
  16.4 0.0 collective-permute-start.10
  16.4 1.3 %setup.1 = (s32[1]{0:T(128)S(4)}, f32[8,128]{1,0:T(8,128)S(1)}, f32[65,8,128]{2,1,0:T(8,128)S(1)}, f32[64,6,8,128]{3,2,1,0:T(8,128)S(1)}) custom-call(s32[1]{0:T(128)} %bitcast.1.base, s32[8,128]{1,0:T(8,128)S(1)} %get-tuple-element.15.active, f32[28,128]{1,0:T(8,128)S(1)} %get-tuple-element.16.own, f32[56,128]{1,0:T(8,128)S(1)} %pad_maximum_fusion.near_by), custom_call_target="tpu_custom_call" | custom-call | tf_op jit(solution)/shard_map/setup/pallas_call | solution.py:271
  17.7 0.0 collective-permute-done.4.rest_1_
  17.7 1.1 %force.3.running = f32[64,6,8,128]{3,2,1,0:T(8,128)S(1)} custom-call(s32[1]{0:T(128)} %bitcast.lead, s32[1]{0:T(128)S(4)} %get-tuple-element.17.count, f32[65,8,128]{2,1,0:T(8,128)S(1)} %get-tuple-element.18.targets, f32[64,6,8,128]{3,2,1,0:T(8,128)S(1)} %get-tuple-element.19.running, ...), custom_call_target="tpu_custom_call", output_to_operand_aliasing={{}: (3, {})} | custom-call | tf_op jit(solution)/shard_map/force/pallas_call | solution.py:295
  18.8 0.0 collective-permute-done.6.rest_1_
  18.8 1.3 %force.4.running = f32[64,6,8,128]{3,2,1,0:T(8,128)S(1)} custom-call(s32[1]{0:T(128)} %bitcast.lead, s32[1]{0:T(128)S(4)} %get-tuple-element.17.count, f32[65,8,128]{2,1,0:T(8,128)S(1)} %get-tuple-element.18.targets, f32[64,6,8,128]{3,2,1,0:T(8,128)S(1)} %force.3.running, ...), custom_call_target="tpu_custom_call", output_to_operand_aliasing={{}: (3, {})} | custom-call | tf_op jit(solution)/shard_map/force/pallas_call | solution.py:295
  20.1 0.0 collective-permute-done.8.rest_1_
  20.2 1.3 %force.5.running = f32[64,6,8,128]{3,2,1,0:T(8,128)S(1)} custom-call(s32[1]{0:T(128)} %bitcast.lead, s32[1]{0:T(128)S(4)} %get-tuple-element.17.count, f32[65,8,128]{2,1,0:T(8,128)S(1)} %get-tuple-element.18.targets, f32[64,6,8,128]{3,2,1,0:T(8,128)S(1)} %force.4.running, ...), custom_call_target="tpu_custom_call", output_to_operand_aliasing={{}: (3, {})} | custom-call | tf_op jit(solution)/shard_map/force/pallas_call | solution.py:295
  21.5 0.0 collective-permute-done.10.rest_1_
  21.5 2.2 %final.1 = (f32[3,512]{1,0:T(4,128)}, f32[3,512]{1,0:T(4,128)}, f32[3,512]{1,0:T(4,128)}, f32[3,512]{1,0:T(4,128)}) custom-call(s32[1]{0:T(128)} %bitcast.lead, s32[1]{0:T(128)S(4)} %get-tuple-element.17.count, f32[65,8,128]{2,1,0:T(8,128)S(1)} %get-tuple-element.18.targets, f32[64,6,8,128]{3,2,1,0:T(8,128)S(1)} %force.5.running, ...), custom_call_target="tpu_custom_call" | custom-call | tf_op jit(solution)/shard_map/final/pallas_call | solution.py:308
  (1 shorter events, 0.0 us)
Async XLA Ops:
  1.4 1.2 %collective-permute-start = (f32[28,128]{1,0:T(8,128)S(1)}, f32[28,128]{1,0:T(8,128)S(1)}, u32[]{:S(2)}, u32[]{:S(2)}) collective-permute-start(f32[28,128]{1,0:T(8,128)S(1)} %get-tuple-element.16.own), channel_id=1, source_target_pairs={{0,4},{1,5},{2,6},{3,7},{4,0},{5,1},{6,2},{7,3},{8,12},{9,13},{10,... | collective-permute-start | bytes 43016 | tf_op jit(solution)/shard_map/ppermute | solution.py:223
  2.7 3.9 %collective-permute-start.1 = (f32[56,128]{1,0:T(8,128)S(1)}, f32[56,128]{1,0:T(8,128)S(1)}, u32[]{:S(2)}, u32[]{:S(2)}) collective-permute-start(f32[56,128]{1,0:T(8,128)S(1)} %pad_maximum_fusion.near_by), channel_id=1, source_target_pairs={{0,8},{1,9},{2,10},{3,11},{4,6},{5,7},{6,4},{7,5},{8,0},{9,1},{10,... | collective-permute-start | bytes 86024 | tf_op jit(solution)/shard_map/ppermute | solution.py:223
  3.3 3.9 %collective-permute-start.2 = (f32[56,128]{1,0:T(8,128)S(1)}, f32[56,128]{1,0:T(8,128)S(1)}, u32[]{:S(2)}, u32[]{:S(2)}) collective-permute-start(f32[56,128]{1,0:T(8,128)S(1)} %pad_maximum_fusion.near_by), channel_id=1, source_target_pairs={{0,8},{1,9},{2,10},{3,11},{4,7},{5,6},{6,5},{7,4},{8,0},{9,1},{10,... | collective-permute-start | bytes 86024 | tf_op jit(solution)/shard_map/ppermute | solution.py:223
  4.8 3.9 %collective-permute-start.3 = (f32[56,128]{1,0:T(8,128)S(1)}, f32[56,128]{1,0:T(8,128)S(1)}, u32[]{:S(2)}, u32[]{:S(2)}) collective-permute-start(f32[56,128]{1,0:T(8,128)S(1)} %pad_maximum_fusion.near_by), channel_id=1, source_target_pairs={{0,8},{1,9},{2,10},{3,11},{4,5},{5,4},{6,7},{7,6},{8,0},{9,1},{10,... | collective-permute-start | bytes 86024 | tf_op jit(solution)/shard_map/ppermute | solution.py:223
  8.7 4.9 %collective-permute-start.5 = (f32[224,128]{1,0:T(8,128)S(1)}, f32[224,128]{1,0:T(8,128)S(1)}, u32[]{:S(2)}, u32[]{:S(2)}) collective-permute-start(f32[224,128]{1,0:T(8,128)S(1)} %concatenate.8.rest_0_), channel_id=1, source_target_pairs={{0,1},{1,0},{2,3},{3,2},{4,12},{5,13},{6,14},{7,15},{8,9},{9,8},{1... | collective-permute-start | bytes 344072 | tf_op jit(solution)/shard_map/ppermute | solution.py:223
  10.4 4.8 %collective-permute-start.7 = (f32[224,128]{1,0:T(8,128)S(1)}, f32[224,128]{1,0:T(8,128)S(1)}, u32[]{:S(2)}, u32[]{:S(2)}) collective-permute-start(f32[224,128]{1,0:T(8,128)S(1)} %concatenate.8.rest_0_), channel_id=1, source_target_pairs={{0,1},{1,0},{2,3},{3,2},{4,20},{5,21},{6,22},{7,23},{8,9},{9,8},{1... | collective-permute-start | bytes 344072 | tf_op jit(solution)/shard_map/ppermute | solution.py:223
  10.8 5.6 %collective-permute-start.9 = (f32[224,128]{1,0:T(8,128)S(1)}, f32[224,128]{1,0:T(8,128)S(1)}, u32[]{:S(2)}, u32[]{:S(2)}) collective-permute-start(f32[224,128]{1,0:T(8,128)S(1)} %concatenate.8.rest_0_), channel_id=1, source_target_pairs={{0,1},{1,0},{2,3},{3,2},{4,28},{5,29},{6,30},{7,31},{8,9},{9,8},{1... | collective-permute-start | bytes 344072 | tf_op jit(solution)/shard_map/ppermute | solution.py:223
  12.4 5.3 %collective-permute-start.4 = (f32[224,128]{1,0:T(8,128)S(1)}, f32[224,128]{1,0:T(8,128)S(1)}, u32[]{:S(2)}, u32[]{:S(2)}) collective-permute-start(f32[224,128]{1,0:T(8,128)S(1)} %concatenate.8.rest_0_), channel_id=1, source_target_pairs={{0,4},{1,5},{2,6},{3,7},{4,0},{5,1},{6,2},{7,3},{8,12},{9,13},{10,... | collective-permute-start | bytes 344072 | tf_op jit(solution)/shard_map/ppermute | solution.py:223
  13.6 5.2 %collective-permute-start.6 = (f32[224,128]{1,0:T(8,128)S(1)}, f32[224,128]{1,0:T(8,128)S(1)}, u32[]{:S(2)}, u32[]{:S(2)}) collective-permute-start(f32[224,128]{1,0:T(8,128)S(1)} %collective-permute-done.5.rest_0_), channel_id=1, source_target_pairs={{0,4},{1,5},{2,6},{3,7},{4,0},{5,1},{6,2},{7,3},{8,12},{9,13},{10,... | collective-permute-start | bytes 344072 | tf_op jit(solution)/shard_map/ppermute | solution.py:223
  15.2 5.0 %collective-permute-start.8 = (f32[224,128]{1,0:T(8,128)S(1)}, f32[224,128]{1,0:T(8,128)S(1)}, u32[]{:S(2)}, u32[]{:S(2)}) collective-permute-start(f32[224,128]{1,0:T(8,128)S(1)} %collective-permute-done.7.rest_0_), channel_id=1, source_target_pairs={{0,4},{1,5},{2,6},{3,7},{4,0},{5,1},{6,2},{7,3},{8,12},{9,13},{10,... | collective-permute-start | bytes 344072 | tf_op jit(solution)/shard_map/ppermute | solution.py:223
  16.4 5.1 %collective-permute-start.10 = (f32[224,128]{1,0:T(8,128)S(1)}, f32[224,128]{1,0:T(8,128)S(1)}, u32[]{:S(2)}, u32[]{:S(2)}) collective-permute-start(f32[224,128]{1,0:T(8,128)S(1)} %collective-permute-done.9.rest_0_), channel_id=1, source_target_pairs={{0,4},{1,5},{2,6},{3,7},{4,0},{5,1},{6,2},{7,3},{8,12},{9,13},{10,... | collective-permute-start | bytes 344072 | tf_op jit(solution)/shard_map/ppermute | solution.py:223

commit v2 on v1

--- a/solution.py
+++ b/solution.py
@@ -45,9 +45,9 @@
     return jnp.broadcast_to(ref[row : row + 1, :], (SUB, LANES))
 
 
-def add_pairs(target, sums, source, first=0):
+def add_pairs(target, sums, source):
     sums = list(sums)
-    for base in range(first, source.shape[0], 7):
+    for base in range(0, source.shape[0], 7):
         sep = [splat_row(source, base + k) - target[k] for k in range(3)]
         rel = [splat_row(source, base + 3 + k) - target[3 + k] for k in range(3)]
         radius_sq = (sep[0] * sep[0] + sep[1] * sep[1]) + (sep[2] * sep[2] + softening)
@@ -66,7 +66,7 @@
     return [jnp.zeros((SUB, LANES), jnp.float32) for _ in range(6)]
 
 
-def setup_body(base, active, own, near_by, count, rank, targets, sums):
+def setup_body(base, active, own, count, rank, targets):
     tiles = own.shape[0] // 7
     rows = max(SUB, tiles)
     sub_rows = lax.broadcasted_iota(jnp.int32, (rows, LANES), 0)
@@ -92,66 +92,45 @@
     total = jnp.sum(flags).astype(jnp.int32)
     count[0] = (total + (SUB - 1)) // SUB
     slot = lax.broadcasted_iota(jnp.int32, (SUB, LANES), 0)
-    lane = lax.broadcasted_iota(jnp.int32, (SUB, LANES), 1)
 
     def fill(c, carry):
         ids = (slot + c * SUB).astype(jnp.float32)
         hits = [ids == splat_row(rank, t) for t in range(tiles)]
-        target = []
-        packed = jnp.zeros((SUB, LANES), jnp.float32)
         for k in range(6):
             found = jnp.zeros((SUB, LANES), jnp.float32)
             for t in range(tiles):
                 found = found + jnp.where(hits[t], splat_row(own, 7 * t + k), 0.0)
-            value = jnp.broadcast_to(jnp.sum(found, axis=1, keepdims=True), (SUB, LANES))
-            packed = jnp.where(lane == k, value, packed)
-            target.append(value)
-        targets[c] = packed
-        for k, value in enumerate(add_pairs(target, zeros6(), near_by)):
-            sums[c, k] = value
+            targets[c, k] = jnp.broadcast_to(jnp.sum(found, axis=1, keepdims=True), (SUB, LANES))
         return carry
 
     lax.fori_loop(0, count[0], fill, 0)
 
 
-def add_piece(first, lead, count, targets, running, sent, got, sums):
-    def unpack(c):
-        packed = targets[c]
-        return tuple(jnp.broadcast_to(packed[:, k : k + 1], (SUB, LANES)) for k in range(6))
-
-    def add_from(source):
-        def chunk(c, target):
-            following = unpack(c + 1)
-            now = add_pairs(target, [running[c, k] for k in range(6)], source, first)
-            for k in range(6):
-                sums[c, k] = now[k]
-            return following
-
-        lax.fori_loop(0, count[0], chunk, unpack(0))
-
-    if got is None:
-        add_from(sent)
-        return
-
-    @pl.when(lead[0] == 1)
-    def from_link():
-        add_from(sent)
-
-    @pl.when(lead[0] != 1)
-    def from_core():
-        add_from(got)
-
-
-def force_body(first, shared, lead, count, targets, running, *rest):
-    sent, got, sums = (rest[0], rest[1], rest[2]) if shared else (rest[0], None, rest[1])
-    add_piece(first, lead, count, targets, running, sent, got, sums)
-
-
-def final_body(first, shared, scale, lead, count, targets, running, *rest):
-    sent, got, rest = (rest[0], rest[1], rest[2:]) if shared else (rest[0], None, rest[1:])
-    rank, pos, vel, acc, jerk, elapsed, new_pos, new_vel, new_acc, new_jerk, sums, landed = rest
+def add_pieces(count, targets, running, sources, sums):
+    def chunk(c, carry):
+        target = [targets[c, k] for k in range(6)]
+        now = zeros6() if running is None else [running[c, k] for k in range(6)]
+        for source in sources:
+            now = add_pairs(target, now, source)
+        for k in range(6):
+            sums[c, k] = now[k]
+        return carry
+
+    lax.fori_loop(0, count[0], chunk, 0)
+
+
+def first_body(count, targets, *rest):
+    add_pieces(count, targets, None, rest[:-1], rest[-1])
+
+
+def force_body(count, targets, running, *rest):
+    add_pieces(count, targets, running, rest[:-1], rest[-1])
+
+
+def final_body(scale, count, targets, running, source, rank, pos, vel, acc, jerk, elapsed, *rest):
+    new_pos, new_vel, new_acc, new_jerk, sums, landed = rest
     tiles = pos.shape[1] // LANES
-    add_piece(first, lead, count, targets, running, sent, got, sums)
+    add_pieces(count, targets, running, [source], sums)
     slot = lax.broadcasted_iota(jnp.int32, (SUB, LANES), 0)
     landed[...] = jnp.zeros(landed.shape, jnp.float32)
 
@@ -199,9 +178,12 @@
     return cores, row_count // cores, col_count
 
 
-def col_order(count):
-    middle = count // 2
-    return ([middle] if middle > 1 else []) + [k for k in range(count - 1, 0, -1) if k != middle or k == 1]
+def col_slots(count, cores):
+    if cores == 1:
+        return [(k, None) for k in range(1, count)]
+    near_by = list(range(1, (count - 1) // 2 + 1))
+    distant = list(range(len(near_by) + 1, count))
+    return list(zip(distant, near_by + [None] * (len(distant) - len(near_by))))
 
 
 def on_device(positions, velocities, accels, jerks, masses, elapsed, active_star):
@@ -222,27 +204,22 @@
                 pairs.append((r * col_count + c, (p * cores + q) * col_count + z))
         return lax.ppermute(value, AXES, pairs)
 
-    def along_col(value, k):
-        to = partner(col_count, k)
+    def along_col(value, ours, theirs):
         idle = partner(plane, 1) if plane > 1 else None
 
         def move(p, q, z):
-            if q == cores - 1 or idle is None:
-                return p, q, to[z]
+            k = ours if q == cores - 1 else theirs
+            if k is not None:
+                return p, q, partner(col_count, k)[z]
+            if idle is None:
+                return p, q, partner(col_count, 1)[z]
             return idle[p], q, z
 
         return send(value, move)
 
     def along_plane(value, k):
         to = partner(plane, k)
-        idle = partner(col_count, 1) if col_count > 1 else None
-
-        def move(p, q, z):
-            if q == cores - 1 or idle is None:
-                return to[p], q, z
-            return p, q, idle[z]
-
-        return send(value, move)
+        return send(value, lambda p, q, z: (to[p], q, z))
 
     def across(value):
         return send(value, lambda p, q, z: (p, 1 - q, z))
@@ -264,59 +241,82 @@
         name="predict",
     )(*map(far, (*state, masses.reshape(1, stars), wide, active)))
 
+    lead = row_index % cores == cores - 1
     chip = jnp.concatenate([own, across(own)], axis=0) if cores == 2 else own
-    found = [along_col(chip, k) for k in col_order(col_count)]
-
-    block = pltpu.VMEM((slots, 6, SUB, LANES), f32)
-    count, rank, targets, sums = pl.pallas_call(
+    slots = col_slots(col_count, cores)
+    half = [along_col(chip, ours, theirs) for ours, theirs in slots]
+    if cores == 2 and slots and slots[-1][1] is None:
+        half[-1] = jnp.where(lead, half[-1], chip)
+    else:
+        half = [own, *half]
+
+    block = pltpu.VMEM((-(-stars // SUB), 6, SUB, LANES), f32)
+    count, rank, targets = pl.pallas_call(
         setup_body,
-        in_specs=[SMEM, VMEM, VMEM, VMEM],
+        in_specs=[SMEM, VMEM, VMEM],
         out_shape=(
             pltpu.SMEM((1,), i32),
             pltpu.VMEM((max(SUB, tiles), LANES), f32),
-            pltpu.VMEM((slots + 1, SUB, LANES), f32),
             block,
         ),
-        out_specs=(SMEM, VMEM, VMEM, VMEM),
+        out_specs=(SMEM, VMEM, VMEM),
         compiler_params=PARAMS,
         name="setup",
-    )((device_id * stars).reshape(1).astype(i32), near(active), near(own), near(chip))
-
-    line = jnp.concatenate([chip, *found], axis=0)
-    pieces = [("line", line, chip.shape[0])]
-    pieces += [(f"plane_{k}", along_plane(line, k), 0) for k in range(1, plane)]
-    shared = cores == 2
-    lead = (row_index % cores == cores - 1).reshape(1).astype(i32)
-    held = []
-    for name, value, first in pieces:
-        both = [value, across(value)] if shared else [value]
-        held.append((name, first, both))
-    for name, first, both in held[:-1]:
+    )((device_id * stars).reshape(1).astype(i32), near(active), near(own))
+
+    half = jnp.concatenate(half, axis=0)
+    held = {"half": half}
+    held.update({f"plane_{k}": along_plane(half, k) for k in plane_order(plane)})
+    if cores == 2:
+        held.update({f"core_{name}": across(value) for name, value in list(held.items())})
+    order = add_order(plane, cores)
+    sums = None
+    for name in order[:-1]:
+        args = (targets, held[name]) if sums is None else (targets, sums, held[name])
         sums = pl.pallas_call(
-            functools.partial(force_body, first, shared),
-            in_specs=[SMEM, SMEM] + [VMEM] * (2 + len(both)),
+            first_body if sums is None else force_body,
+            in_specs=[SMEM] + [VMEM] * len(args),
             out_shape=block,
             out_specs=VMEM,
-            input_output_aliases={3: 0},
+            input_output_aliases={} if sums is None else {2: 0},
             compiler_params=PARAMS,
             name="force",
-        )(lead, count, near(targets), near(sums), *map(near, both))
-
-    name, first, both = held[-1]
+        )(count, *map(near, args))
+
     shape = jax.ShapeDtypeStruct(positions.shape, f32)
-    near_args = (targets, sums, *both, rank, *kept, wide)
+    if sums is None:
+        sums = jnp.zeros(block.shape, f32)
+    near_args = (targets, sums, held[order[-1]], rank, *kept, wide)
     return pl.pallas_call(
-        functools.partial(final_body, first, shared, scale),
-        in_specs=[SMEM, SMEM] + [VMEM] * len(near_args),
+        functools.partial(final_body, scale),
+        in_specs=[SMEM] + [VMEM] * len(near_args),
         out_shape=(shape, shape, shape, shape),
         out_specs=(VMEM, VMEM, VMEM, VMEM),
         scratch_shapes=[
-            pltpu.VMEM((slots + GROUP, 6, SUB, LANES), f32),
+            pltpu.VMEM((block.shape[0] + GROUP, 6, SUB, LANES), f32),
             pltpu.VMEM((tiles, 6, SUB, LANES), f32),
         ],
         compiler_params=PARAMS,
         name="final",
-    )(lead, count, *map(near, near_args))
+    )(count, *map(near, near_args))
+
+
+def plane_order(plane):
+    return list(range(2, plane)) + ([1] if plane > 1 else [])
+
+
+def add_order(plane, cores):
+    planes = [f"plane_{k}" for k in plane_order(plane)]
+    if cores == 1:
+        return ["half", *planes]
+    order = ["half", "core_half"]
+    for i, name in enumerate(planes):
+        order.append(name)
+        if i + 1 < len(planes):
+            order.append(f"core_{name}")
+    if len(planes) > 1:
+        order[-2:] = [f"core_{planes[-2]}", planes[-1]]
+    return order + [f"core_{name}" for name in planes[-1:]]
 
 
 def solution(mesh):

time: 23.9 us -> 23 us (0.962)
  the two profiles are of different devices: /device:TPU:18 before, /device:TPU:1 now
where the time goes in v2:
time: 23 us; the launch traced here: 22.8 us
  starting transfers between devices  7.85 us (34%)
  waiting for transfers between devices  7.78 us (34%)
  Pallas kernels  6.43 us (28%)
  between operations  0.71 us (3%)
    ppermute x10, starting transfers between devices, send(): return lax.ppermute(value, AXES, pairs)  7.85 us
    ppermute x10, waiting for transfers between devices, send(): return lax.ppermute(value, AXES, pairs)  7.78 us
    pallas_call x7, Pallas kernels, on_device(): pl.pallas_call(first_body if sums is None else force_body, in_specs=[SMEM...  3.4 us
    pallas_call x1, Pallas kernels, on_device(): pl.pallas_call(functools.partial(final_body, scale), in_specs=[SMEM] + [V...  1.41 us
    pallas_call x1, Pallas kernels, on_device(): pl.pallas_call(setup_body, in_specs=[SMEM, VMEM, VMEM], out_shape=(pltpu....  0.81 us
    pallas_call x1, Pallas kernels, on_device(): pl.pallas_call(predict_body, out_shape=(pltpu.VMEM((7 * tiles, LANES), f3...  0.81 us
  transfers between devices with their start and end apart: 10, of which 5 were waited for; matrix products, arithmetic and copies ran while one was open for 0% of the time, Pallas kernels for 18%

profile of v2, /device:TPU:1, one launch (start us, length us, event | category | flops | bytes accessed | tf_op | source)
XLA Modules:
  0.0 22.8 jit_solution(11301076457690788165)
XLA Ops:
  0.6 0.8 %predict.1 = (f32[28,128]{1,0:T(8,128)S(1)}, f32[3,512]{1,0:T(4,128)S(1)}, f32[3,512]{1,0:T(4,128)S(1)}, f32[3,512]{1,0:T(4,128)S(1)}, f32[3,512]{1,0:T(4,128)S(...) custom-call(f32[3,512]{1,0:T(4,128)} %pos.1, f32[3,512]{1,0:T(4,128)} %vel.1, f32[3,512]{1,0:T(4,128)} %acc.1, ...), custom_call_target="tpu_custom_call" | custom-call | tf_op jit(solution)/shard_map/predict/pallas_call | solution.py:232
  1.4 0.1 collective-permute-start
  1.5 1.2 %collective-permute-done = f32[28,128]{1,0:T(8,128)S(1)} collective-permute-done((f32[28,128]{1,0:T(8,128)S(1)}, f32[28,128]{1,0:T(8,128)S(1)}, u32[]{:S(2)}, u32[]{:S(2)}) %collective-permute-start) | collective-permute-done | bytes 14368 | tf_op jit(solution)/shard_map/ppermute | solution.py:205
  2.7 4.5 %collective-permute-start.2 = (f32[56,128]{1,0:T(8,128)S(1)}, f32[56,128]{1,0:T(8,128)S(1)}, u32[]{:S(2)}, u32[]{:S(2)}) collective-permute-start(f32[56,128]{1,0:T(8,128)S(1)} %pad_maximum_fusion.1), channel_id=1, source_target_pairs={{0,8},{1,9},{2,10},{3,11},{4,7},{5,6},{6,5},{7,4},{8,0},{9,1},{10,... | collective-permute-start | bytes 86024 | tf_op jit(solution)/shard_map/ppermute | solution.py:205
  7.2 0.0 collective-permute-start.1
  7.2 1.3 %collective-permute-done.2 = f32[56,128]{1,0:T(8,128)S(1)} collective-permute-done((f32[56,128]{1,0:T(8,128)S(1)}, f32[56,128]{1,0:T(8,128)S(1)}, u32[]{:S(2)}, u32[]{:S(2)}) %collective-permute-start.2) | collective-permute-done | bytes 28704 | tf_op jit(solution)/shard_map/ppermute | solution.py:205
  8.4 2.4 %collective-permute-done.1 = f32[56,128]{1,0:T(8,128)S(1)} collective-permute-done((f32[56,128]{1,0:T(8,128)S(1)}, f32[56,128]{1,0:T(8,128)S(1)}, u32[]{:S(2)}, u32[]{:S(2)}) %collective-permute-start.1) | collective-permute-done | bytes 28704 | tf_op jit(solution)/shard_map/ppermute | solution.py:205
  10.8 1.2 %collective-permute-start.4 = (f32[112,128]{1,0:T(8,128)S(1)}, f32[112,128]{1,0:T(8,128)S(1)}, u32[]{:S(2)}, u32[]{:S(2)}) collective-permute-start(f32[112,128]{1,0:T(8,128)S(1)} %pad_maximum_fusion.rest_0_), channel_id=1, source_target_pairs={{0,16},{1,17},{2,18},{3,19},{4,20},{5,21},{6,22},{7,23},{8,24},{9,... | collective-permute-start | bytes 172040 | tf_op jit(solution)/shard_map/ppermute | solution.py:205
  12.0 1.2 %collective-permute-start.6 = (f32[112,128]{1,0:T(8,128)S(1)}, f32[112,128]{1,0:T(8,128)S(1)}, u32[]{:S(2)}, u32[]{:S(2)}) collective-permute-start(f32[112,128]{1,0:T(8,128)S(1)} %pad_maximum_fusion.rest_0_), channel_id=1, source_target_pairs={{0,24},{1,25},{2,26},{3,27},{4,28},{5,29},{6,30},{7,31},{8,16},{9,... | collective-permute-start | bytes 172040 | tf_op jit(solution)/shard_map/ppermute | solution.py:205
  13.2 0.3 %collective-permute-start.8 = (f32[112,128]{1,0:T(8,128)S(1)}, f32[112,128]{1,0:T(8,128)S(1)}, u32[]{:S(2)}, u32[]{:S(2)}) collective-permute-start(f32[112,128]{1,0:T(8,128)S(1)} %pad_maximum_fusion.rest_0_), channel_id=1, source_target_pairs={{0,8},{1,9},{2,10},{3,11},{4,12},{5,13},{6,14},{7,15},{8,0},{9,1},... | collective-permute-start | bytes 172040 | tf_op jit(solution)/shard_map/ppermute | solution.py:205
  13.4 0.0 collective-permute-start.3
  13.5 0.4 %collective-permute-done.4.rest_0_ = f32[112,128]{1,0:T(8,128)S(1)} collective-permute-done((f32[112,128]{1,0:T(8,128)S(1)}, f32[112,128]{1,0:T(8,128)S(1)}, u32[]{:S(2)}, u32[]{:S(2)}) %collective-permute-start.4) | collective-permute-done | bytes 57376 | tf_op jit(solution)/shard_map/ppermute | solution.py:205
  13.8 0.1 collective-permute-start.5
  14.0 2.6 %collective-permute-done.6.rest_0_ = f32[112,128]{1,0:T(8,128)S(1)} collective-permute-done((f32[112,128]{1,0:T(8,128)S(1)}, f32[112,128]{1,0:T(8,128)S(1)}, u32[]{:S(2)}, u32[]{:S(2)}) %collective-permute-start.6) | collective-permute-done | bytes 57376 | tf_op jit(solution)/shard_map/ppermute | solution.py:205
  16.6 0.0 collective-permute-start.7
  16.6 0.0 collective-permute-done.8.rest_0_
  16.6 0.5 %collective-permute-start.9 = (f32[112,128]{1,0:T(8,128)S(1)}, f32[112,128]{1,0:T(8,128)S(1)}, u32[]{:S(2)}, u32[]{:S(2)}) collective-permute-start(f32[112,128]{1,0:T(8,128)S(1)} %collective-permute-done.8.rest_0_), channel_id=1, source_target_pairs={{0,4},{1,5},{2,6},{3,7},{4,0},{5,1},{6,2},{7,3},{8,12},{9,13},{10,... | collective-permute-start | bytes 172040 | tf_op jit(solution)/shard_map/ppermute | solution.py:205
  17.1 0.8 %setup.1 = (s32[1]{0:T(128)S(4)}, f32[8,128]{1,0:T(8,128)S(1)}, f32[64,6,8,128]{3,2,1,0:T(8,128)S(1)}) custom-call(s32[1]{0:T(128)} %bitcast.base, s32[8,128]{1,0:T(8,128)S(1)} %get-tuple-element.14.active, f32[28,128]{1,0:T(8,128)S(1)} %get-tuple-element.15.own), custom_call_target="tpu_custom_call" | custom-call | tf_op jit(solution)/shard_map/setup/pallas_call | solution.py:254
  17.9 0.5 %force.7.running = f32[64,6,8,128]{3,2,1,0:T(8,128)S(1)} custom-call(s32[1]{0:T(128)S(4)} %get-tuple-element.16.count, f32[64,6,8,128]{3,2,1,0:T(8,128)S(1)} %get-tuple-element.17.targets, f32[112,128]{1,0:T(8,128)S(1)} %pad_maximum_fusion.rest_0_), custom_call_target="tpu_custom_call" | custom-call | tf_op jit(solution)/shard_map/force/pallas_call | solution.py:276
  18.4 0.0 collective-permute-done.3.rest_0_
  18.4 0.5 %force.8.running = f32[64,6,8,128]{3,2,1,0:T(8,128)S(1)} custom-call(s32[1]{0:T(128)S(4)} %get-tuple-element.16.count, f32[64,6,8,128]{3,2,1,0:T(8,128)S(1)} %get-tuple-element.17.targets, f32[64,6,8,128]{3,2,1,0:T(8,128)S(1)} %force.7.running, f32[112,128]{1,0:T(8,128)S(1)} %collective-permute-done.3.rest_0_), custom_call_target="tpu_custom_call", output_to_operand_aliasing={{}: (2, {})} | custom-call | tf_op jit(solution)/shard_map/force/pallas_call | solution.py:276
  18.9 0.5 %force.9.running = f32[64,6,8,128]{3,2,1,0:T(8,128)S(1)} custom-call(s32[1]{0:T(128)S(4)} %get-tuple-element.16.count, f32[64,6,8,128]{3,2,1,0:T(8,128)S(1)} %get-tuple-element.17.targets, f32[64,6,8,128]{3,2,1,0:T(8,128)S(1)} %force.8.running, f32[112,128]{1,0:T(8,128)S(1)} %collective-permute-done.4.rest_0_), custom_call_target="tpu_custom_call", output_to_operand_aliasing={{}: (2, {})} | custom-call | tf_op jit(solution)/shard_map/force/pallas_call | solution.py:276
  19.4 0.0 collective-permute-done.5.rest_0_
  19.4 0.5 %force.10.running = f32[64,6,8,128]{3,2,1,0:T(8,128)S(1)} custom-call(s32[1]{0:T(128)S(4)} %get-tuple-element.16.count, f32[64,6,8,128]{3,2,1,0:T(8,128)S(1)} %get-tuple-element.17.targets, f32[64,6,8,128]{3,2,1,0:T(8,128)S(1)} %force.9.running, f32[112,128]{1,0:T(8,128)S(1)} %collective-permute-done.5.rest_0_), custom_call_target="tpu_custom_call", output_to_operand_aliasing={{}: (2, {})} | custom-call | tf_op jit(solution)/shard_map/force/pallas_call | solution.py:276
  19.9 0.5 %force.11.running = f32[64,6,8,128]{3,2,1,0:T(8,128)S(1)} custom-call(s32[1]{0:T(128)S(4)} %get-tuple-element.16.count, f32[64,6,8,128]{3,2,1,0:T(8,128)S(1)} %get-tuple-element.17.targets, f32[64,6,8,128]{3,2,1,0:T(8,128)S(1)} %force.10.running, f32[112,128]{1,0:T(8,128)S(1)} %collective-permute-done.6.rest_0_), custom_call_target="tpu_custom_call", output_to_operand_aliasing={{}: (2, {})} | custom-call | tf_op jit(solution)/shard_map/force/pallas_call | solution.py:276
  20.4 0.0 collective-permute-done.7.rest_0_
  20.4 0.5 %force.12.running = f32[64,6,8,128]{3,2,1,0:T(8,128)S(1)} custom-call(s32[1]{0:T(128)S(4)} %get-tuple-element.16.count, f32[64,6,8,128]{3,2,1,0:T(8,128)S(1)} %get-tuple-element.17.targets, f32[64,6,8,128]{3,2,1,0:T(8,128)S(1)} %force.11.running, f32[112,128]{1,0:T(8,128)S(1)} %collective-permute-done.7.rest_0_), custom_call_target="tpu_custom_call", output_to_operand_aliasing={{}: (2, {})} | custom-call | tf_op jit(solution)/shard_map/force/pallas_call | solution.py:276
  20.9 0.5 %force.13.running = f32[64,6,8,128]{3,2,1,0:T(8,128)S(1)} custom-call(s32[1]{0:T(128)S(4)} %get-tuple-element.16.count, f32[64,6,8,128]{3,2,1,0:T(8,128)S(1)} %get-tuple-element.17.targets, f32[64,6,8,128]{3,2,1,0:T(8,128)S(1)} %force.12.running, f32[112,128]{1,0:T(8,128)S(1)} %collective-permute-done.8.rest_0_), custom_call_target="tpu_custom_call", output_to_operand_aliasing={{}: (2, {})} | custom-call | tf_op jit(solution)/shard_map/force/pallas_call | solution.py:276
  21.4 0.0 collective-permute-done.9.source
  21.4 1.4 %final.1 = (f32[3,512]{1,0:T(4,128)}, f32[3,512]{1,0:T(4,128)}, f32[3,512]{1,0:T(4,128)}, f32[3,512]{1,0:T(4,128)}) custom-call(s32[1]{0:T(128)S(4)} %get-tuple-element.16.count, f32[64,6,8,128]{3,2,1,0:T(8,128)S(1)} %get-tuple-element.17.targets, f32[64,6,8,128]{3,2,1,0:T(8,128)S(1)} %force.13.running, f32[112,128]{1,0:T(8,128)S(1)} %collective-permute-done.9.source, ...), custom_call_target="tpu_custom_call" | custom-call | tf_op jit(solution)/shard_map/final/pallas_call | solution.py:290
  (3 shorter events, 0.0 us)
Async XLA Ops:
  1.4 1.2 %collective-permute-start = (f32[28,128]{1,0:T(8,128)S(1)}, f32[28,128]{1,0:T(8,128)S(1)}, u32[]{:S(2)}, u32[]{:S(2)}) collective-permute-start(f32[28,128]{1,0:T(8,128)S(1)} %get-tuple-element.15.own), channel_id=1, source_target_pairs={{0,4},{1,5},{2,6},{3,7},{4,0},{5,1},{6,2},{7,3},{8,12},{9,13},{10,... | collective-permute-start | bytes 43016 | tf_op jit(solution)/shard_map/ppermute | solution.py:205
  2.7 5.7 %collective-permute-start.2 = (f32[56,128]{1,0:T(8,128)S(1)}, f32[56,128]{1,0:T(8,128)S(1)}, u32[]{:S(2)}, u32[]{:S(2)}) collective-permute-start(f32[56,128]{1,0:T(8,128)S(1)} %pad_maximum_fusion.1), channel_id=1, source_target_pairs={{0,8},{1,9},{2,10},{3,11},{4,7},{5,6},{6,5},{7,4},{8,0},{9,1},{10,... | collective-permute-start | bytes 86024 | tf_op jit(solution)/shard_map/ppermute | solution.py:205
  7.2 3.6 %collective-permute-start.1 = (f32[56,128]{1,0:T(8,128)S(1)}, f32[56,128]{1,0:T(8,128)S(1)}, u32[]{:S(2)}, u32[]{:S(2)}) collective-permute-start(f32[56,128]{1,0:T(8,128)S(1)} %pad_maximum_fusion.1), channel_id=1, source_target_pairs={{0,1},{1,0},{2,3},{3,2},{4,6},{5,7},{6,4},{7,5},{8,9},{9,8},{10,11... | collective-permute-start | bytes 86024 | tf_op jit(solution)/shard_map/ppermute | solution.py:205
  10.8 3.0 %collective-permute-start.4 = (f32[112,128]{1,0:T(8,128)S(1)}, f32[112,128]{1,0:T(8,128)S(1)}, u32[]{:S(2)}, u32[]{:S(2)}) collective-permute-start(f32[112,128]{1,0:T(8,128)S(1)} %pad_maximum_fusion.rest_0_), channel_id=1, source_target_pairs={{0,16},{1,17},{2,18},{3,19},{4,20},{5,21},{6,22},{7,23},{8,24},{9,... | collective-permute-start | bytes 172040 | tf_op jit(solution)/shard_map/ppermute | solution.py:205
  12.0 4.5 %collective-permute-start.6 = (f32[112,128]{1,0:T(8,128)S(1)}, f32[112,128]{1,0:T(8,128)S(1)}, u32[]{:S(2)}, u32[]{:S(2)}) collective-permute-start(f32[112,128]{1,0:T(8,128)S(1)} %pad_maximum_fusion.rest_0_), channel_id=1, source_target_pairs={{0,24},{1,25},{2,26},{3,27},{4,28},{5,29},{6,30},{7,31},{8,16},{9,... | collective-permute-start | bytes 172040 | tf_op jit(solution)/shard_map/ppermute | solution.py:205
  13.2 3.4 %collective-permute-start.8 = (f32[112,128]{1,0:T(8,128)S(1)}, f32[112,128]{1,0:T(8,128)S(1)}, u32[]{:S(2)}, u32[]{:S(2)}) collective-permute-start(f32[112,128]{1,0:T(8,128)S(1)} %pad_maximum_fusion.rest_0_), channel_id=1, source_target_pairs={{0,8},{1,9},{2,10},{3,11},{4,12},{5,13},{6,14},{7,15},{8,0},{9,1},... | collective-permute-start | bytes 172040 | tf_op jit(solution)/shard_map/ppermute | solution.py:205
  13.4 5.0 %collective-permute-start.3 = (f32[112,128]{1,0:T(8,128)S(1)}, f32[112,128]{1,0:T(8,128)S(1)}, u32[]{:S(2)}, u32[]{:S(2)}) collective-permute-start(f32[112,128]{1,0:T(8,128)S(1)} %pad_maximum_fusion.rest_0_), channel_id=1, source_target_pairs={{0,4},{1,5},{2,6},{3,7},{4,0},{5,1},{6,2},{7,3},{8,12},{9,13},{10,... | collective-permute-start | bytes 172040 | tf_op jit(solution)/shard_map/ppermute | solution.py:205
  13.8 5.6 %collective-permute-start.5 = (f32[112,128]{1,0:T(8,128)S(1)}, f32[112,128]{1,0:T(8,128)S(1)}, u32[]{:S(2)}, u32[]{:S(2)}) collective-permute-start(f32[112,128]{1,0:T(8,128)S(1)} %collective-permute-done.4.rest_0_), channel_id=1, source_target_pairs={{0,4},{1,5},{2,6},{3,7},{4,0},{5,1},{6,2},{7,3},{8,12},{9,13},{10,... | collective-permute-start | bytes 172040 | tf_op jit(solution)/shard_map/ppermute | solution.py:205
  16.6 3.8 %collective-permute-start.7 = (f32[112,128]{1,0:T(8,128)S(1)}, f32[112,128]{1,0:T(8,128)S(1)}, u32[]{:S(2)}, u32[]{:S(2)}) collective-permute-start(f32[112,128]{1,0:T(8,128)S(1)} %collective-permute-done.6.rest_0_), channel_id=1, source_target_pairs={{0,4},{1,5},{2,6},{3,7},{4,0},{5,1},{6,2},{7,3},{8,12},{9,13},{10,... | collective-permute-start | bytes 172040 | tf_op jit(solution)/shard_map/ppermute | solution.py:205
  16.6 4.8 %collective-permute-start.9 = (f32[112,128]{1,0:T(8,128)S(1)}, f32[112,128]{1,0:T(8,128)S(1)}, u32[]{:S(2)}, u32[]{:S(2)}) collective-permute-start(f32[112,128]{1,0:T(8,128)S(1)} %collective-permute-done.8.rest_0_), channel_id=1, source_target_pairs={{0,4},{1,5},{2,6},{3,7},{4,0},{5,1},{6,2},{7,3},{8,12},{9,13},{10,... | collective-permute-start | bytes 172040 | tf_op jit(solution)/shard_map/ppermute | solution.py:205

commit v3 on v2

--- a/solution.py
+++ b/solution.py
@@ -119,6 +119,16 @@
     lax.fori_loop(0, count[0], chunk, 0)
 
 
+def line_body(shared, lead, count, targets, running, swapped, fetched, sums):
+    @pl.when(lead[0] == 1)
+    def on_lead():
+        add_pieces(count, targets, running, [swapped.at[0:shared], fetched], sums)
+
+    @pl.when(lead[0] != 1)
+    def on_other():
+        add_pieces(count, targets, running, [swapped], sums)
+
+
 def first_body(count, targets, *rest):
     add_pieces(count, targets, None, rest[:-1], rest[-1])
 
@@ -135,21 +145,23 @@
     landed[...] = jnp.zeros(landed.shape, jnp.float32)
 
     def land(g, carry):
+        forces, hits = [], []
         for c in range(GROUP):
             chunk = g * GROUP + c
             ids = (slot + chunk * SUB).astype(jnp.float32)
-            hits = [ids == splat_row(rank, t) for t in range(tiles)]
-            for k in range(6):
-                total = jnp.sum(sums[chunk, k], axis=1, keepdims=True)
-                force = jnp.broadcast_to(total, (SUB, LANES)) * scale
-                for t in range(tiles):
-                    landed[t, k] += jnp.where(hits[t], force, 0.0)
+            hits.append([ids == splat_row(rank, t) for t in range(tiles)])
+            sides = [jnp.sum(sums[chunk, k], axis=1, keepdims=True) for k in range(6)]
+            forces.append([jnp.broadcast_to(side, (SUB, LANES)) for side in sides])
+        for k in range(6):
+            for t in range(tiles):
+                found = [jnp.where(hits[c][t], forces[c][k], 0.0) for c in range(GROUP)]
+                landed[t, k] += functools.reduce(jnp.add, found)
         return carry
 
     lax.fori_loop(0, (count[0] + (GROUP - 1)) // GROUP, land, 0)
     for t in range(tiles):
         lanes = slice(t * LANES, (t + 1) * LANES)
-        force = [jnp.sum(landed[t, k], axis=0, keepdims=True) for k in range(6)]
+        force = [jnp.sum(landed[t, k], axis=0, keepdims=True) * scale for k in range(6)]
         acc_now = jnp.concatenate(force[0:3], axis=0)
         jerk_now = jnp.concatenate(force[3:6], axis=0)
         hit = jnp.broadcast_to(rank[t : t + 1, :], (3, LANES)) >= 0.0
@@ -206,9 +218,12 @@
 
     def along_col(value, ours, theirs):
         idle = partner(plane, 1) if plane > 1 else None
+        crossed = cores == 2 and col_count >= 4 and col_count & (col_count - 1) == 0
 
         def move(p, q, z):
             k = ours if q == cores - 1 else theirs
+            if crossed and q == cores - 1 and z >= col_count // 2:
+                k = ours ^ 1
             if k is not None:
                 return p, q, partner(col_count, k)[z]
             if idle is None:
@@ -244,11 +259,13 @@
     lead = row_index % cores == cores - 1
     chip = jnp.concatenate([own, across(own)], axis=0) if cores == 2 else own
     slots = col_slots(col_count, cores)
-    half = [along_col(chip, ours, theirs) for ours, theirs in slots]
-    if cores == 2 and slots and slots[-1][1] is None:
-        half[-1] = jnp.where(lead, half[-1], chip)
+    fetched = [along_col(chip, ours, theirs) for ours, theirs in slots]
+    split = cores == 2 and len(slots) > 0 and slots[-1][1] is None
+    if split:
+        first = [chip, *fetched[:-1]]
+        half = [*fetched[:-1], jnp.where(lead, fetched[-1], chip)]
     else:
-        half = [own, *half]
+        first = half = [own, *fetched]
 
     block = pltpu.VMEM((-(-stars // SUB), 6, SUB, LANES), f32)
     count, rank, targets = pl.pallas_call(
@@ -269,23 +286,31 @@
     held.update({f"plane_{k}": along_plane(half, k) for k in plane_order(plane)})
     if cores == 2:
         held.update({f"core_{name}": across(value) for name, value in list(held.items())})
-    order = add_order(plane, cores)
-    sums = None
-    for name in order[:-1]:
-        args = (targets, held[name]) if sums is None else (targets, sums, held[name])
-        sums = pl.pallas_call(
-            first_body if sums is None else force_body,
-            in_specs=[SMEM] + [VMEM] * len(args),
+
+    def add(body, sums, *sources, flags=()):
+        args = (targets, *sources) if sums is None else (targets, sums, *sources)
+        return pl.pallas_call(
+            body,
+            in_specs=[SMEM] * (1 + len(flags)) + [VMEM] * len(args),
             out_shape=block,
             out_specs=VMEM,
-            input_output_aliases={} if sums is None else {2: 0},
+            input_output_aliases={} if sums is None else {2 + len(flags): 0},
             compiler_params=PARAMS,
             name="force",
-        )(count, *map(near, args))
+        )(*flags, count, *map(near, args))
+
+    sums = add(first_body, None, *first)
+    order = add_order(plane, cores)
+    for name in order[:-1]:
+        if name == "core_half" and split:
+            flag = lead.reshape(1).astype(i32)
+            shared = half.shape[0] - chip.shape[0]
+            body = functools.partial(line_body, shared)
+            sums = add(body, sums, held[name], fetched[-1], flags=(flag,))
+        else:
+            sums = add(force_body, sums, held[name])
 
     shape = jax.ShapeDtypeStruct(positions.shape, f32)
-    if sums is None:
-        sums = jnp.zeros(block.shape, f32)
     near_args = (targets, sums, held[order[-1]], rank, *kept, wide)
     return pl.pallas_call(
         functools.partial(final_body, scale),
@@ -308,8 +333,8 @@
 def add_order(plane, cores):
     planes = [f"plane_{k}" for k in plane_order(plane)]
     if cores == 1:
-        return ["half", *planes]
-    order = ["half", "core_half"]
+        return planes
+    order = ["core_half"]
     for i, name in enumerate(planes):
         order.append(name)
         if i + 1 < len(planes):

time: 23 us -> 23.3 us (1.013)
  waiting for transfers between devices: 7.78 us -> 8.45 us
  starting transfers between devices: 7.85 us -> 7.47 us
    ppermute x10, waiting for transfers between devices: 7.78 us -> 8.45 us  [send(): return lax.ppermute(value, AXES, pairs)]
    ppermute x10, starting transfers between devices: 7.85 us -> 7.47 us  [send(): return lax.ppermute(value, AXES, pairs)]
  transfers between devices with their start and end apart: 10 -> 10, of which waited for: 5 -> 6; matrix products, arithmetic and copies ran while one was open for 0% -> 0% of each run, Pallas kernels for 18% -> 18%
where the time goes in v3:
time: 23.3 us; the launch traced here: 23.1 us
  waiting for transfers between devices  8.45 us (36%)
  starting transfers between devices  7.47 us (32%)
  Pallas kernels  6.46 us (28%)
  between operations  0.71 us (3%)
    ppermute x10, waiting for transfers between devices, send(): return lax.ppermute(value, AXES, pairs)  8.45 us
    ppermute x10, starting transfers between devices, send(): return lax.ppermute(value, AXES, pairs)  7.47 us
    pallas_call x7, Pallas kernels, add(): pl.pallas_call(body, in_specs=[SMEM] * (1 + len(flags)) + [VMEM] * len(ar...  3.43 us
    pallas_call x1, Pallas kernels, on_device(): pl.pallas_call(functools.partial(final_body, scale), in_specs=[SMEM] + [V...  1.41 us
    pallas_call x1, Pallas kernels, on_device(): pl.pallas_call(setup_body, in_specs=[SMEM, VMEM, VMEM], out_shape=(pltpu....  0.81 us
    pallas_call x1, Pallas kernels, on_device(): pl.pallas_call(predict_body, out_shape=(pltpu.VMEM((7 * tiles, LANES), f3...  0.81 us
  transfers between devices with their start and end apart: 10, of which 6 were waited for; matrix products, arithmetic and copies ran while one was open for 0% of the time, Pallas kernels for 18%

profile of v3, /device:TPU:1, one launch (start us, length us, event | category | flops | bytes accessed | tf_op | source)
XLA Modules:
  0.0 23.1 jit_solution(4034216341779960798)
XLA Ops:
  0.6 0.8 %predict.1 = (f32[28,128]{1,0:T(8,128)S(1)}, f32[3,512]{1,0:T(4,128)S(1)}, f32[3,512]{1,0:T(4,128)S(1)}, f32[3,512]{1,0:T(4,128)S(1)}, f32[3,512]{1,0:T(4,128)S(...) custom-call(f32[3,512]{1,0:T(4,128)} %pos.1, f32[3,512]{1,0:T(4,128)} %vel.1, f32[3,512]{1,0:T(4,128)} %acc.1, ...), custom_call_target="tpu_custom_call" | custom-call | tf_op jit(solution)/shard_map/predict/pallas_call | solution.py:247
  1.4 0.1 collective-permute-start
  1.5 1.2 %collective-permute-done = f32[28,128]{1,0:T(8,128)S(1)} collective-permute-done((f32[28,128]{1,0:T(8,128)S(1)}, f32[28,128]{1,0:T(8,128)S(1)}, u32[]{:S(2)}, u32[]{:S(2)}) %collective-permute-start) | collective-permute-done | bytes 14368 | tf_op jit(solution)/shard_map/ppermute | solution.py:217
  2.7 4.5 %collective-permute-start.2 = (f32[56,128]{1,0:T(8,128)S(1)}, f32[56,128]{1,0:T(8,128)S(1)}, u32[]{:S(2)}, u32[]{:S(2)}) collective-permute-start(f32[56,128]{1,0:T(8,128)S(1)} %pad_maximum_fusion.1.rest_0_), channel_id=1, source_target_pairs={{0,8},{1,9},{2,10},{3,11},{4,7},{5,6},{6,4},{7,5},{8,0},{9,1},{10,... | collective-permute-start | bytes 86024 | tf_op jit(solution)/shard_map/ppermute | solution.py:217
  7.2 0.0 collective-permute-start.1
  7.2 1.0 %collective-permute-done.2.fetched = f32[56,128]{1,0:T(8,128)S(1)} collective-permute-done((f32[56,128]{1,0:T(8,128)S(1)}, f32[56,128]{1,0:T(8,128)S(1)}, u32[]{:S(2)}, u32[]{:S(2)}) %collective-permute-start.2) | collective-permute-done | bytes 28704 | tf_op jit(solution)/shard_map/ppermute | solution.py:217
  8.2 3.5 %collective-permute-done.1.rest_1_ = f32[56,128]{1,0:T(8,128)S(1)} collective-permute-done((f32[56,128]{1,0:T(8,128)S(1)}, f32[56,128]{1,0:T(8,128)S(1)}, u32[]{:S(2)}, u32[]{:S(2)}) %collective-permute-start.1) | collective-permute-done | bytes 28704 | tf_op jit(solution)/shard_map/ppermute | solution.py:217
  11.7 1.2 %collective-permute-start.4 = (f32[112,128]{1,0:T(8,128)S(1)}, f32[112,128]{1,0:T(8,128)S(1)}, u32[]{:S(2)}, u32[]{:S(2)}) collective-permute-start(f32[112,128]{1,0:T(8,128)S(1)} %pad_maximum_fusion), channel_id=1, source_target_pairs={{0,16},{1,17},{2,18},{3,19},{4,20},{5,21},{6,22},{7,23},{8,24},{9,... | collective-permute-start | bytes 172040 | tf_op jit(solution)/shard_map/ppermute | solution.py:217
  12.9 1.2 %collective-permute-start.6 = (f32[112,128]{1,0:T(8,128)S(1)}, f32[112,128]{1,0:T(8,128)S(1)}, u32[]{:S(2)}, u32[]{:S(2)}) collective-permute-start(f32[112,128]{1,0:T(8,128)S(1)} %pad_maximum_fusion), channel_id=1, source_target_pairs={{0,24},{1,25},{2,26},{3,27},{4,28},{5,29},{6,30},{7,31},{8,16},{9,... | collective-permute-start | bytes 172040 | tf_op jit(solution)/shard_map/ppermute | solution.py:217
  14.1 0.3 %collective-permute-start.8 = (f32[112,128]{1,0:T(8,128)S(1)}, f32[112,128]{1,0:T(8,128)S(1)}, u32[]{:S(2)}, u32[]{:S(2)}) collective-permute-start(f32[112,128]{1,0:T(8,128)S(1)} %pad_maximum_fusion), channel_id=1, source_target_pairs={{0,8},{1,9},{2,10},{3,11},{4,12},{5,13},{6,14},{7,15},{8,0},{9,1},... | collective-permute-start | bytes 172040 | tf_op jit(solution)/shard_map/ppermute | solution.py:217
  14.3 0.0 collective-permute-start.3
  14.4 0.7 %collective-permute-done.4.rest_0_ = f32[112,128]{1,0:T(8,128)S(1)} collective-permute-done((f32[112,128]{1,0:T(8,128)S(1)}, f32[112,128]{1,0:T(8,128)S(1)}, u32[]{:S(2)}, u32[]{:S(2)}) %collective-permute-start.4) | collective-permute-done | bytes 57376 | tf_op jit(solution)/shard_map/ppermute | solution.py:217
  15.0 0.0 collective-permute-start.5
  15.0 1.8 %collective-permute-done.6.rest_0_ = f32[112,128]{1,0:T(8,128)S(1)} collective-permute-done((f32[112,128]{1,0:T(8,128)S(1)}, f32[112,128]{1,0:T(8,128)S(1)}, u32[]{:S(2)}, u32[]{:S(2)}) %collective-permute-start.6) | collective-permute-done | bytes 57376 | tf_op jit(solution)/shard_map/ppermute | solution.py:217
  16.9 0.0 collective-permute-start.7
  16.9 0.3 %collective-permute-done.8.rest_0_ = f32[112,128]{1,0:T(8,128)S(1)} collective-permute-done((f32[112,128]{1,0:T(8,128)S(1)}, f32[112,128]{1,0:T(8,128)S(1)}, u32[]{:S(2)}, u32[]{:S(2)}) %collective-permute-start.8) | collective-permute-done | bytes 57376 | tf_op jit(solution)/shard_map/ppermute | solution.py:217
  17.1 0.3 %collective-permute-start.9 = (f32[112,128]{1,0:T(8,128)S(1)}, f32[112,128]{1,0:T(8,128)S(1)}, u32[]{:S(2)}, u32[]{:S(2)}) collective-permute-start(f32[112,128]{1,0:T(8,128)S(1)} %collective-permute-done.8.rest_0_), channel_id=1, source_target_pairs={{0,4},{1,5},{2,6},{3,7},{4,0},{5,1},{6,2},{7,3},{8,12},{9,13},{10,... | collective-permute-start | bytes 172040 | tf_op jit(solution)/shard_map/ppermute | solution.py:217
  17.4 0.8 %setup.1 = (s32[1]{0:T(128)S(4)}, f32[8,128]{1,0:T(8,128)S(1)}, f32[64,6,8,128]{3,2,1,0:T(8,128)S(1)}) custom-call(s32[1]{0:T(128)} %bitcast.base, s32[8,128]{1,0:T(8,128)S(1)} %get-tuple-element.14.active, f32[28,128]{1,0:T(8,128)S(1)} %get-tuple-element.15.own), custom_call_target="tpu_custom_call" | custom-call | tf_op jit(solution)/shard_map/setup/pallas_call | solution.py:271
  18.2 0.5 %force.7.running = f32[64,6,8,128]{3,2,1,0:T(8,128)S(1)} custom-call(s32[1]{0:T(128)S(4)} %get-tuple-element.16.count, f32[64,6,8,128]{3,2,1,0:T(8,128)S(1)} %get-tuple-element.17.targets, f32[56,128]{1,0:T(8,128)S(1)} %pad_maximum_fusion.1.rest_0_, f32[56,128]{1,0:T(8,128)S(1)} %collective-permute-done.1.rest_1_), custom_call_target="tpu_custom_call" | custom-call | tf_op jit(solution)/shard_map/force/pallas_call | solution.py:292
  18.7 0.0 collective-permute-done.3.swapped
  18.7 0.5 %force.8.running = f32[64,6,8,128]{3,2,1,0:T(8,128)S(1)} custom-call(s32[1]{0:T(128)} %bitcast.4.lead, s32[1]{0:T(128)S(4)} %get-tuple-element.16.count, f32[64,6,8,128]{3,2,1,0:T(8,128)S(1)} %get-tuple-element.17.targets, f32[64,6,8,128]{3,2,1,0:T(8,128)S(1)} %force.7.running, ...), custom_call_target="tpu_custom_call", output_to_operand_aliasing={{}: (3, {})} | custom-call | tf_op jit(solution)/shard_map/force/pallas_call | solution.py:292
  19.2 0.5 %force.9.running = f32[64,6,8,128]{3,2,1,0:T(8,128)S(1)} custom-call(s32[1]{0:T(128)S(4)} %get-tuple-element.16.count, f32[64,6,8,128]{3,2,1,0:T(8,128)S(1)} %get-tuple-element.17.targets, f32[64,6,8,128]{3,2,1,0:T(8,128)S(1)} %force.8.running, f32[112,128]{1,0:T(8,128)S(1)} %collective-permute-done.4.rest_0_), custom_call_target="tpu_custom_call", output_to_operand_aliasing={{}: (2, {})} | custom-call | tf_op jit(solution)/shard_map/force/pallas_call | solution.py:292
  19.7 0.0 collective-permute-done.5.rest_0_
  19.7 0.5 %force.10.running = f32[64,6,8,128]{3,2,1,0:T(8,128)S(1)} custom-call(s32[1]{0:T(128)S(4)} %get-tuple-element.16.count, f32[64,6,8,128]{3,2,1,0:T(8,128)S(1)} %get-tuple-element.17.targets, f32[64,6,8,128]{3,2,1,0:T(8,128)S(1)} %force.9.running, f32[112,128]{1,0:T(8,128)S(1)} %collective-permute-done.5.rest_0_), custom_call_target="tpu_custom_call", output_to_operand_aliasing={{}: (2, {})} | custom-call | tf_op jit(solution)/shard_map/force/pallas_call | solution.py:292
  20.2 0.5 %force.11.running = f32[64,6,8,128]{3,2,1,0:T(8,128)S(1)} custom-call(s32[1]{0:T(128)S(4)} %get-tuple-element.16.count, f32[64,6,8,128]{3,2,1,0:T(8,128)S(1)} %get-tuple-element.17.targets, f32[64,6,8,128]{3,2,1,0:T(8,128)S(1)} %force.10.running, f32[112,128]{1,0:T(8,128)S(1)} %collective-permute-done.6.rest_0_), custom_call_target="tpu_custom_call", output_to_operand_aliasing={{}: (2, {})} | custom-call | tf_op jit(solution)/shard_map/force/pallas_call | solution.py:292
  20.7 0.0 collective-permute-done.7.rest_0_
  20.7 0.5 %force.12.running = f32[64,6,8,128]{3,2,1,0:T(8,128)S(1)} custom-call(s32[1]{0:T(128)S(4)} %get-tuple-element.16.count, f32[64,6,8,128]{3,2,1,0:T(8,128)S(1)} %get-tuple-element.17.targets, f32[64,6,8,128]{3,2,1,0:T(8,128)S(1)} %force.11.running, f32[112,128]{1,0:T(8,128)S(1)} %collective-permute-done.7.rest_0_), custom_call_target="tpu_custom_call", output_to_operand_aliasing={{}: (2, {})} | custom-call | tf_op jit(solution)/shard_map/force/pallas_call | solution.py:292
  21.2 0.5 %force.13.running = f32[64,6,8,128]{3,2,1,0:T(8,128)S(1)} custom-call(s32[1]{0:T(128)S(4)} %get-tuple-element.16.count, f32[64,6,8,128]{3,2,1,0:T(8,128)S(1)} %get-tuple-element.17.targets, f32[64,6,8,128]{3,2,1,0:T(8,128)S(1)} %force.12.running, f32[112,128]{1,0:T(8,128)S(1)} %collective-permute-done.8.rest_0_), custom_call_target="tpu_custom_call", output_to_operand_aliasing={{}: (2, {})} | custom-call | tf_op jit(solution)/shard_map/force/pallas_call | solution.py:292
  21.7 0.0 collective-permute-done.9.source
  21.7 1.4 %final.1 = (f32[3,512]{1,0:T(4,128)}, f32[3,512]{1,0:T(4,128)}, f32[3,512]{1,0:T(4,128)}, f32[3,512]{1,0:T(4,128)}) custom-call(s32[1]{0:T(128)S(4)} %get-tuple-element.16.count, f32[64,6,8,128]{3,2,1,0:T(8,128)S(1)} %get-tuple-element.17.targets, f32[64,6,8,128]{3,2,1,0:T(8,128)S(1)} %force.13.running, f32[112,128]{1,0:T(8,128)S(1)} %collective-permute-done.9.source, ...), custom_call_target="tpu_custom_call" | custom-call | tf_op jit(solution)/shard_map/final/pallas_call | solution.py:315
  (3 shorter events, 0.0 us)
Async XLA Ops:
  1.4 1.2 %collective-permute-start = (f32[28,128]{1,0:T(8,128)S(1)}, f32[28,128]{1,0:T(8,128)S(1)}, u32[]{:S(2)}, u32[]{:S(2)}) collective-permute-start(f32[28,128]{1,0:T(8,128)S(1)} %get-tuple-element.15.own), channel_id=1, source_target_pairs={{0,4},{1,5},{2,6},{3,7},{4,0},{5,1},{6,2},{7,3},{8,12},{9,13},{10,... | collective-permute-start | bytes 43016 | tf_op jit(solution)/shard_map/ppermute | solution.py:217
  2.7 5.5 %collective-permute-start.2 = (f32[56,128]{1,0:T(8,128)S(1)}, f32[56,128]{1,0:T(8,128)S(1)}, u32[]{:S(2)}, u32[]{:S(2)}) collective-permute-start(f32[56,128]{1,0:T(8,128)S(1)} %pad_maximum_fusion.1.rest_0_), channel_id=1, source_target_pairs={{0,8},{1,9},{2,10},{3,11},{4,7},{5,6},{6,4},{7,5},{8,0},{9,1},{10,... | collective-permute-start | bytes 86024 | tf_op jit(solution)/shard_map/ppermute | solution.py:217
  7.2 4.5 %collective-permute-start.1 = (f32[56,128]{1,0:T(8,128)S(1)}, f32[56,128]{1,0:T(8,128)S(1)}, u32[]{:S(2)}, u32[]{:S(2)}) collective-permute-start(f32[56,128]{1,0:T(8,128)S(1)} %pad_maximum_fusion.1.rest_0_), channel_id=1, source_target_pairs={{0,1},{1,0},{2,3},{3,2},{4,6},{5,7},{6,5},{7,4},{8,9},{9,8},{10,11... | collective-permute-start | bytes 86024 | tf_op jit(solution)/shard_map/ppermute | solution.py:217
  11.7 3.3 %collective-permute-start.4 = (f32[112,128]{1,0:T(8,128)S(1)}, f32[112,128]{1,0:T(8,128)S(1)}, u32[]{:S(2)}, u32[]{:S(2)}) collective-permute-start(f32[112,128]{1,0:T(8,128)S(1)} %pad_maximum_fusion), channel_id=1, source_target_pairs={{0,16},{1,17},{2,18},{3,19},{4,20},{5,21},{6,22},{7,23},{8,24},{9,... | collective-permute-start | bytes 172040 | tf_op jit(solution)/shard_map/ppermute | solution.py:217
  12.9 3.9 %collective-permute-start.6 = (f32[112,128]{1,0:T(8,128)S(1)}, f32[112,128]{1,0:T(8,128)S(1)}, u32[]{:S(2)}, u32[]{:S(2)}) collective-permute-start(f32[112,128]{1,0:T(8,128)S(1)} %pad_maximum_fusion), channel_id=1, source_target_pairs={{0,24},{1,25},{2,26},{3,27},{4,28},{5,29},{6,30},{7,31},{8,16},{9,... | collective-permute-start | bytes 172040 | tf_op jit(solution)/shard_map/ppermute | solution.py:217
  14.1 3.0 %collective-permute-start.8 = (f32[112,128]{1,0:T(8,128)S(1)}, f32[112,128]{1,0:T(8,128)S(1)}, u32[]{:S(2)}, u32[]{:S(2)}) collective-permute-start(f32[112,128]{1,0:T(8,128)S(1)} %pad_maximum_fusion), channel_id=1, source_target_pairs={{0,8},{1,9},{2,10},{3,11},{4,12},{5,13},{6,14},{7,15},{8,0},{9,1},... | collective-permute-start | bytes 172040 | tf_op jit(solution)/shard_map/ppermute | solution.py:217
  14.3 4.4 %collective-permute-start.3 = (f32[112,128]{1,0:T(8,128)S(1)}, f32[112,128]{1,0:T(8,128)S(1)}, u32[]{:S(2)}, u32[]{:S(2)}) collective-permute-start(f32[112,128]{1,0:T(8,128)S(1)} %pad_maximum_fusion), channel_id=1, source_target_pairs={{0,4},{1,5},{2,6},{3,7},{4,0},{5,1},{6,2},{7,3},{8,12},{9,13},{10,... | collective-permute-start | bytes 172040 | tf_op jit(solution)/shard_map/ppermute | solution.py:217
  15.0 4.7 %collective-permute-start.5 = (f32[112,128]{1,0:T(8,128)S(1)}, f32[112,128]{1,0:T(8,128)S(1)}, u32[]{:S(2)}, u32[]{:S(2)}) collective-permute-start(f32[112,128]{1,0:T(8,128)S(1)} %collective-permute-done.4.rest_0_), channel_id=1, source_target_pairs={{0,4},{1,5},{2,6},{3,7},{4,0},{5,1},{6,2},{7,3},{8,12},{9,13},{10,... | collective-permute-start | bytes 172040 | tf_op jit(solution)/shard_map/ppermute | solution.py:217
  16.9 3.8 %collective-permute-start.7 = (f32[112,128]{1,0:T(8,128)S(1)}, f32[112,128]{1,0:T(8,128)S(1)}, u32[]{:S(2)}, u32[]{:S(2)}) collective-permute-start(f32[112,128]{1,0:T(8,128)S(1)} %collective-permute-done.6.rest_0_), channel_id=1, source_target_pairs={{0,4},{1,5},{2,6},{3,7},{4,0},{5,1},{6,2},{7,3},{8,12},{9,13},{10,... | collective-permute-start | bytes 172040 | tf_op jit(solution)/shard_map/ppermute | solution.py:217
  17.1 4.6 %collective-permute-start.9 = (f32[112,128]{1,0:T(8,128)S(1)}, f32[112,128]{1,0:T(8,128)S(1)}, u32[]{:S(2)}, u32[]{:S(2)}) collective-permute-start(f32[112,128]{1,0:T(8,128)S(1)} %collective-permute-done.8.rest_0_), channel_id=1, source_target_pairs={{0,4},{1,5},{2,6},{3,7},{4,0},{5,1},{6,2},{7,3},{8,12},{9,13},{10,... | collective-permute-start | bytes 172040 | tf_op jit(solution)/shard_map/ppermute | solution.py:217
